TPU v7x, 256 devices: a whole 4x4x8 slice. The times are simulated.
256 devices in a mesh: seq: 32 (over x, z_hi, core), ch: 8 (over z_lo, y).
Axes of the slice: x: 4, y: 4, z: 8 (z_hi: 4, z_lo: 2; z = z_hi * 2 + z_lo), core: 2. Of those that a mesh axis runs over, the one named last changes fastest.
Arguments:
- queries: bfloat16 [8192, 4096], P('seq', 'ch'), may hold values from -6 to 6
- key_in: bfloat16 [8192, 4096], P('seq', 'ch'), may hold values from -6 to 6
- value_in: bfloat16 [8192, 4096], P('seq', 'ch'), may hold values from -6 to 6
- filter_raw: bfloat16 [8192, 4096], P('seq', 'ch'), may hold values from -6 to 6
- skip_gain: float32 [4096], P('ch'), may hold values from -4 to 4
- out_weight: bfloat16 [4096, 4096], P('ch'), may hold values from -0.09375 to 0.09375
- cotangent: bfloat16 [8192, 4096], P('seq', 'ch'), may hold values from -6 to 6
Outputs:
- projected: bfloat16 [8192, 4096], P('seq', 'ch')
- grad_query: bfloat16 [8192, 4096], P('seq', 'ch')
- grad_key: bfloat16 [8192, 4096], P('seq', 'ch')
- grad_value: bfloat16 [8192, 4096], P('seq', 'ch')
- grad_filter: bfloat16 [8192, 4096], P('seq', 'ch')
All inputs are finite; a program needn't handle non-finite values.
Results may differ from a plain program's by a relative error of at most 0.015.
Values may be sent and summed in bfloat16 or wider, within the bound.
No kernel may reach another device: no remote copies, remote signals or barrier semaphores. Data moves between devices by JAX's collectives and lax.ppermute only.
A program may use at most 128 MiB of HBM per device.

v0:
```python
import functools
import math

import jax
import jax.numpy as jnp
import numpy as np
from jax import lax
from jax.experimental import pallas as pl
from jax.experimental.pallas import tpu as pltpu
from jax.sharding import PartitionSpec as P


bf16 = jnp.bfloat16
f32 = jnp.float32
LANES = 128


def split(table):
    high = table.astype(bf16)
    low = (table - high.astype(np.float64)).astype(bf16)
    return np.asarray(high), np.asarray(low)


def tables(length, devices):
    points = 2 * length
    half = points // LANES // 2
    parts = half // devices
    rows = np.arange(half)
    j = parts * (rows % devices) + rows // devices
    k1 = np.arange(half) + 0.5
    lanes = np.arange(LANES)
    angle = 2.0 * np.pi / (2 * half) * np.outer(k1, j)
    first = np.concatenate([np.cos(angle), -np.sin(angle)], 0)
    last = np.concatenate([np.cos(angle.T), -np.sin(angle.T)], 1)
    turn = 2.0 * np.pi / points * np.outer(k1, lanes)
    factor = 2.0 / (points * math.sqrt(length))
    turns = np.stack([np.cos(turn), -np.sin(turn), np.cos(turn) * factor, np.sin(turn) * factor])
    phase = 2.0 * np.pi / LANES * (np.outer(lanes, lanes) % LANES)
    c, s = np.cos(phase), np.sin(phase)
    over = np.block([[c, -s], [s, c]])
    under = np.block([[c, s], [-s, c]])
    first_high, first_low = split(first)
    last_high, last_low = split(last)
    return (
        np.concatenate([first_high, first_low], 0),
        np.stack(split(over)),
        np.stack(split(under)),
        np.concatenate([last_high, last_low], 0),
        turns.astype(np.float32),
    )


def dot(a, b):
    return lax.dot_general(a, b, (((1,), (0,)), ((), ())), preferred_element_type=f32)


def halves(x):
    high = x.astype(bf16)
    return high, (x - high.astype(f32)).astype(bf16)


def forward(x, first, turns):
    half = turns.shape[1]
    both = dot(first, x)
    a = both[: 2 * half] + both[2 * half :]
    real, imag = a[:half], a[half:]
    return jnp.concatenate(
        [real * turns[0] - imag * turns[1], real * turns[1] + imag * turns[0]], 1
    )


def lanes_dot(x, table):
    high, low = halves(x)
    return dot(high, table[0]) + dot(low, table[0]) + dot(high, table[1])


def backward(b, last, turns):
    real, imag = b[:, :LANES], b[:, LANES:]
    d = jnp.concatenate([real * turns[2] - imag * turns[3], real * turns[3] + imag * turns[2]], 0)
    high, low = halves(d)
    rows = last.shape[0] // 2
    both = dot(last, high)
    return both[:rows] + both[rows:] + dot(last[:rows], low)


def product(a, b, conjugate):
    ar, ai = a[:, :LANES], a[:, LANES:]
    br, bi = b[:, :LANES], b[:, LANES:]
    if conjugate:
        return jnp.concatenate([ar * br + ai * bi, ar * bi - ai * br], 1)
    return jnp.concatenate([ar * br - ai * bi, ar * bi + ai * br], 1)


def fetch(pairs, sems):
    copies = [pltpu.make_async_copy(a, b, sems.at[i]) for i, (a, b) in enumerate(pairs)]
    for copy in copies:
        copy.start()
    return copies


def prepare_body(key_hbm, value_hbm, filter_hbm, out_ref, pkv_ref, key_ref, value_ref, filter_ref, sems):
    copies = fetch([(key_hbm, key_ref), (value_hbm, value_ref), (filter_hbm, filter_ref)], sems)
    peers, _, width, local_rows = out_ref.shape
    copies[0].wait()
    copies[1].wait()
    pkv = (key_ref[...].astype(f32) * value_ref[...].astype(f32)).astype(bf16)
    pkv_ref[...] = pkv
    out_ref[:, 0] = pkv.T.reshape(peers, width, local_rows)
    copies[2].wait()
    out_ref[:, 1] = filter_ref[...].T.reshape(peers, width, local_rows)


def spread(x, rows_ref):
    for p in range(rows_ref.shape[0]):
        part = x[:, :, p * LANES : (p + 1) * LANES]
        rows_ref[p] = part.astype(f32).reshape(rows_ref.shape[1:])


def gather(rows_ref, out_ref, s):
    for p in range(rows_ref.shape[0]):
        part = rows_ref[p].reshape(*out_ref.shape[:1], *out_ref.shape[-2:-1], LANES).astype(bf16)
        if s is None:
            out_ref[:, :, p * LANES : (p + 1) * LANES] = part
        else:
            out_ref[:, s, :, p * LANES : (p + 1) * LANES] = part


def channel(rows_ref, c, devices, width):
    parts = [rows_ref[p, pl.ds(c, devices, stride=width), :] for p in range(rows_ref.shape[0])]
    return jnp.concatenate(parts, 0).astype(bf16)


def put_channel(rows_ref, c, devices, width, y):
    for p in range(rows_ref.shape[0]):
        rows_ref[p, pl.ds(c, devices, stride=width), :] = y[p * devices : (p + 1) * devices]


def conv_body(
    x_ref, first_hbm, turns_hbm, over_hbm, under_hbm, last_hbm, out_ref, spec_ref,
    a_ref, rows_ref, first_ref, turns_ref, over_ref, under_ref, last_ref, sems,
):
    copies = fetch(
        [
            (first_hbm, first_ref),
            (turns_hbm, turns_ref),
            (over_hbm, over_ref),
            (under_hbm, under_ref),
            (last_hbm, last_ref),
        ],
        sems,
    )
    devices, _, width, _ = x_ref.shape
    half = turns_ref.shape[1]
    for s in range(2):
        spread(x_ref[:, s], rows_ref)
        if s == 0:
            copies[0].wait()
            copies[1].wait()
        for c in range(width):
            x = channel(rows_ref, c, devices, width)
            a_ref[s, c] = forward(x, first_ref[...], turns_ref)
    for copy in copies[2:]:
        copy.wait()
    spectra = lanes_dot(a_ref[...].reshape(2 * width * half, 2 * LANES), over_ref)
    spec_ref[...] = spectra.reshape(spec_ref.shape)
    for c in range(width):
        a_ref[0, c] = product(spec_ref[1, c], spec_ref[0, c], False)
    b = lanes_dot(a_ref[0].reshape(width * half, 2 * LANES), under_ref)
    a_ref[1] = b.reshape(width, half, 2 * LANES)
    for c in range(width):
        y = backward(a_ref[1, c], last_ref[...], turns_ref)
        put_channel(rows_ref, c, devices, width, y)
    gather(rows_ref, out_ref, None)


def back_body(
    x_ref, spec_ref, first_hbm, turns_hbm, over_hbm, under_hbm, last_hbm, out_ref,
    a_ref, rows_ref, first_ref, turns_ref, over_ref, under_ref, last_ref, sems,
):
    copies = fetch(
        [
            (first_hbm, first_ref),
            (turns_hbm, turns_ref),
            (over_hbm, over_ref),
            (under_hbm, under_ref),
            (last_hbm, last_ref),
        ],
        sems,
    )
    devices, _, width, _ = x_ref.shape
    half = turns_ref.shape[1]
    spread(x_ref[:, 1], rows_ref)
    copies[0].wait()
    copies[1].wait()
    for c in range(width):
        x = channel(rows_ref, c, devices, width)
        a_ref[0, c] = forward(x, first_ref[...], turns_ref)
    for copy in copies[2:]:
        copy.wait()
    g = lanes_dot(a_ref[0].reshape(width * half, 2 * LANES), over_ref)
    a_ref[0] = g.reshape(width, half, 2 * LANES)
    for c in range(width):
        g_c = a_ref[0, c]
        a_ref[1, c] = product(spec_ref[0, c], g_c, True)
        a_ref[0, c] = product(spec_ref[1, c], g_c, True)
    b = lanes_dot(a_ref[...].reshape(2 * width * half, 2 * LANES), under_ref)
    a_ref[...] = b.reshape(a_ref.shape)
    for s in range(2):
        for c in range(width):
            y = backward(a_ref[s, c], last_ref[...], turns_ref)
            put_channel(rows_ref, c, devices, width, y)
        gather(rows_ref, out_ref, s)


def peer(index, near, flip, shift):
    return (index // near + flip) % 2 * near + (index % near + shift) % near


def weight_pairs(weight_hbm, weight_ref, flip, signed_hops):
    here = lax.axis_index("ch")
    near = len(signed_hops)
    width = weight_ref.shape[2]
    pairs = []
    for k, d in enumerate(signed_hops):
        start = pl.multiple_of(peer(here, near, flip, d + near) * width, width)
        pairs.append((weight_hbm.at[:, pl.ds(start, width)], weight_ref.at[k]))
    return pairs


def mixed_terms(copies, weight_ref, parts):
    total = None
    for k, part in enumerate(parts):
        copies[k].wait()
        term = lax.dot_general(
            part[...], weight_ref[k], (((1,), (1,)), ((), ())), preferred_element_type=f32
        )
        total = term if total is None else total + term
    return total


def mixed_body(hops, weight_hbm, own_hbm, *refs):
    *parts, out_ref, own_ref, weight_ref, sems = refs
    pairs = [(own_hbm, own_ref)] + weight_pairs(weight_hbm, weight_ref, 0, [-d for d in hops])
    copies = fetch(pairs, sems)
    copies[0].wait()
    out_ref[...] = mixed_terms(copies[1:], weight_ref, [own_ref] + parts)


def conv_grad_body(hops, weight_hbm, queries_hbm, before_ref, forward_ref, *refs):
    *parts, mixed_ref, conv_ref, sent_ref, queries_ref, weight_ref, sems = refs
    pairs = weight_pairs(weight_hbm, weight_ref, 1, [-d for d in hops])
    copies = fetch(pairs + [(queries_hbm, queries_ref)], sems)
    sent_ref[:, 0] = forward_ref[...]
    mixed = before_ref[...] + mixed_terms(copies, weight_ref, parts)
    mixed_ref[...] = mixed
    copies[-1].wait()
    g = (mixed * queries_ref[...].astype(f32)).astype(bf16)
    conv_ref[...] = g
    sent_ref[:, 1] = g.T.reshape(forward_ref.shape)


def project(copies, weight_ref, gated, out_refs):
    for k, out_ref in enumerate(out_refs):
        copies[k].wait()
        out_ref[...] = dot(gated, weight_ref[k]).astype(bf16)


def gate_body(hops, weight_hbm, queries_hbm, conv_ref, pkv_ref, skip_ref, *refs):
    convolved_ref, gated_ref, *out_refs, queries_ref, weight_ref, sems = refs
    pairs = weight_pairs(weight_hbm, weight_ref, 1, hops)
    copies = fetch([(queries_hbm, queries_ref)] + pairs, sems)
    local_rows = queries_ref.shape[0]
    conv = conv_ref[:, 0].reshape(-1, local_rows).T.astype(f32)
    convolved = conv + skip_ref[...] * pkv_ref[...].astype(f32)
    convolved_ref[...] = convolved
    copies[0].wait()
    gated = (queries_ref[...].astype(f32) * convolved).astype(bf16)
    gated_ref[...] = gated
    project(copies[1:], weight_ref, gated, out_refs)


def project_body(hops, weight_hbm, gated_ref, *refs):
    *out_refs, weight_ref, sems = refs
    copies = fetch(weight_pairs(weight_hbm, weight_ref, 0, hops), sems)
    project(copies, weight_ref, gated_ref[...], out_refs)


def finish_body(res_ref, conv_ref, skip_ref, key_ref, value_ref, gk_ref, gv_ref, gf_ref):
    local_rows = key_ref.shape[0]
    gf_ref[...] = res_ref[:, 1].reshape(-1, local_rows).T
    product_grad = res_ref[:, 0].reshape(-1, local_rows).T.astype(f32)
    product_grad = product_grad + skip_ref[...] * conv_ref[...].astype(f32)
    gk_ref[...] = (product_grad * value_ref[...].astype(f32)).astype(bf16)
    gv_ref[...] = (product_grad * key_ref[...].astype(f32)).astype(bf16)


def call(body, operands, results, scratch=(), flops=1 << 20, hbm=(), copies=0, limit=16):
    vmem = pl.BlockSpec(memory_space=pltpu.VMEM)
    left = pl.BlockSpec(memory_space=pltpu.HBM)
    scratch = list(scratch)
    if copies:
        scratch.append(pltpu.SemaphoreType.DMA((copies,)))
    kernel = pl.pallas_call(
        body,
        in_specs=[left if i in hbm else vmem for i in range(len(operands))],
        out_specs=[vmem] * len(results),
        out_shape=[jax.ShapeDtypeStruct(dims, kind) for dims, kind in results],
        scratch_shapes=scratch,
        cost_estimate=pl.CostEstimate(flops=flops, transcendentals=0, bytes_accessed=4 << 20),
        compiler_params=pltpu.CompilerParams(vmem_limit_bytes=limit << 20),
    )
    stay = pltpu.with_memory_space_constraint
    return list(kernel(*(stay(x, pltpu.HBM) if i in hbm else x for i, x in enumerate(operands))))


def to_all(x, axis):
    return lax.all_to_all(x, axis, split_axis=0, concat_axis=0, tiled=True)


def step(queries, key_in, value_in, filter_raw, skip_gain, out_weight, cotangent):
    local_rows, local_width = queries.shape
    seq_devices = lax.axis_size("seq")
    ch_devices = lax.axis_size("ch")
    length = local_rows * seq_devices
    width = local_width // seq_devices
    half = length // LANES
    first, over, under, last, turns = [jnp.asarray(t) for t in tables(length, seq_devices)]
    table = (first, turns, over, under, last)
    skip = skip_gain.reshape(1, local_width)
    message = (seq_devices, width, local_rows)
    pair = (seq_devices, 2, width, local_rows)
    flat = queries.shape
    near = ch_devices // 2
    work = [
        pltpu.VMEM((2, width, half, 2 * LANES), f32),
        pltpu.VMEM((local_rows // LANES, seq_devices * width, LANES), f32),
    ] + [pltpu.VMEM(t.shape, t.dtype) for t in table]
    own = pltpu.VMEM(flat, bf16)
    weights = pltpu.VMEM((near, local_width, local_width), bf16)

    def move(x, flip, shift):
        pairs = [(i, peer(i, near, flip, shift)) for i in range(ch_devices)]
        return lax.ppermute(x, "ch", pairs)

    hops = sorted(range(1, near), key=lambda d: -min(d, near - d))
    places = [0] + hops
    body = lambda f: functools.partial(f, places)

    other = move(cotangent, 1, 0)
    own_parts = [move(cotangent, 0, d) for d in hops]
    sent, pkv = call(
        prepare_body,
        (key_in, value_in, filter_raw),
        [(pair, bf16), (flat, bf16)],
        [own] * 3,
        hbm=(0, 1, 2),
        copies=3,
    )
    signals = to_all(sent, "seq")
    other_parts = [other] + [move(other, 0, d) for d in hops]

    (mixed,) = call(
        body(mixed_body),
        (out_weight, cotangent, *own_parts),
        [(flat, f32)],
        [own, weights],
        1 << 30,
        hbm=(0, 1),
        copies=1 + near,
    )
    conv, spectra = call(
        conv_body,
        (signals, *table),
        [(message, bf16), ((2, width, half, 2 * LANES), f32)],
        work,
        1 << 31,
        hbm=range(1, 6),
        copies=5,
    )
    mixed, grad_conv, both = call(
        body(conv_grad_body),
        (out_weight, queries, mixed, conv, *other_parts),
        [(flat, f32), (flat, bf16), (pair, bf16)],
        [own, weights],
        1 << 30,
        hbm=(0, 1),
        copies=1 + near,
    )
    both = to_all(both, "seq")

    convolved, gated, *far_terms = call(
        body(gate_body),
        (out_weight, queries, both, pkv, skip),
        [(flat, f32), (flat, bf16)] + [(flat, bf16)] * near,
        [own, weights],
        1 << 30,
        hbm=(0, 1),
        copies=1 + near,
    )
    far_terms = far_terms[:1] + [move(x, 0, d) for x, d in zip(far_terms[1:], hops)]
    near_terms = call(
        body(project_body),
        (out_weight, gated),
        [(flat, bf16)] * near,
        [weights],
        1 << 30,
        hbm=(0,),
        copies=near,
    )
    near_terms = near_terms[:1] + [move(x, 0, d) for x, d in zip(near_terms[1:], hops)]
    (results,) = call(
        back_body,
        (both, spectra, *table),
        [(pair, bf16)],
        work,
        1 << 31,
        hbm=range(2, 7),
        copies=5,
    )
    results = to_all(results, "seq")

    total = lambda terms: sum(x.astype(f32) for x in terms)
    across = move(total(far_terms).astype(bf16), 1, 0)
    grad_query = (mixed * convolved).astype(bf16)
    grad_key, grad_value, grad_filter = call(
        finish_body, (results, grad_conv, skip, key_in, value_in), [(flat, bf16)] * 3
    )
    projected = total(near_terms + [across]).astype(bf16)
    return (projected, grad_query, grad_key, grad_value, grad_filter)


def solution(mesh):
    placed = (
        P("seq", "ch"),
        P("seq", "ch"),
        P("seq", "ch"),
        P("seq", "ch"),
        P("ch"),
        P("ch", None),
        P("seq", "ch"),
    )
    return jax.shard_map(
        step,
        mesh=mesh,
        in_specs=placed,
        out_specs=(P("seq", "ch"),) * 5,
        check_vma=False,
    )
```

profile of v0, /device:TPU:1, one launch (start us, length us, event | category | flops | bytes accessed | tf_op | source)
XLA Modules:
  0.0 119.1 jit_solution(11987486206827388396)
XLA Ops:
  0.6 2.1 %shard_map.156 = (bf16[32,2,16,256]{3,2,1,0:T(8,128)(2,1)}, bf16[256,512]{1,0:T(8,128)(2,1)S(1)}) custom-call(bf16[256,512]{1,0:T(8,128)(2,1)} %key_ref.1, bf16[256,512]{1,0:T(8,128)(2,1)} %value_ref.1, bf16[256,512]{1,0:T(8,128)(2,1)} %filter_hbm.1), custom_call_target="tpu_custom_call" | custom-call | flops 1048576 | bytes 4194304 | tf_op jit(solution)/shard_map/pallas_call | solution.py:313
  2.7 12.6 %all-to-all-start = ((bf16[32,2,16,256]{3,2,1,0:T(8,128)(2,1)}), bf16[32,2,16,256]{3,2,1,0:T(8,128)(2,1)S(1)}, u32[]{:S(2)}, u32[]{:S(2)}) async-start(bf16[32,2,16,256]{3,2,1,0:T(8,128)(2,1)} %get-tuple-element.25), calls=%async_computation | async-start | bytes 1048576 | tf_op jit(solution)/shard_map/all_to_all | solution.py:317
  15.3 0.8 collective-permute-start.3
  16.2 2.7 %collective-permute-start.2 = (bf16[256,512]{1,0:T(8,128)(2,1)}, bf16[256,512]{1,0:T(8,128)(2,1)S(1)}, u32[]{:S(2)}, u32[]{:S(2)}) collective-permute-start(bf16[256,512]{1,0:T(8,128)(2,1)} %own_hbm.1), channel_id=1, source_target_pairs={{0,3},{1,0},{2,1},{3,2},{4,7},{5,4},{6,5},{7,6},{8,11},{9,8},{10,9... | collective-permute-start | bytes 786440 | tf_op jit(solution)/shard_map/ppermute | solution.py:343
  18.9 0.0 collective-permute-start.1
  18.9 1.6 %collective-permute-start = (bf16[256,512]{1,0:T(8,128)(2,1)}, bf16[256,512]{1,0:T(8,128)(2,1)S(1)}, u32[]{:S(2)}, u32[]{:S(2)}) collective-permute-start(bf16[256,512]{1,0:T(8,128)(2,1)} %own_hbm.1), channel_id=1, source_target_pairs={{0,2},{1,3},{2,0},{3,1},{4,6},{5,7},{6,4},{7,5},{8,10},{9,11},{10,... | collective-permute-start | bytes 786440 | tf_op jit(solution)/shard_map/ppermute | solution.py:343
  20.5 13.5 %collective-permute-done.3.refs_0_ = bf16[256,512]{1,0:T(8,128)(2,1)S(1)} collective-permute-done((bf16[256,512]{1,0:T(8,128)(2,1)}, bf16[256,512]{1,0:T(8,128)(2,1)S(1)}, u32[]{:S(2)}, u32[]{:S(2)}) %collective-permute-start.3) | collective-permute-done | bytes 262176 | tf_op jit(solution)/shard_map/ppermute | solution.py:343
  34.0 2.7 %collective-permute-start.6 = (bf16[256,512]{1,0:T(8,128)(2,1)S(1)}, bf16[256,512]{1,0:T(8,128)(2,1)S(1)}, u32[]{:S(2)}, u32[]{:S(2)}) collective-permute-start(bf16[256,512]{1,0:T(8,128)(2,1)S(1)} %collective-permute-done.3.refs_0_), channel_id=1, source_target_pairs={{0,3},{1,0},{2,1},{3,2},{4,7},{5,4},{6,5},{7,6},{8,11},{9,8},{10,9... | collective-permute-start | bytes 786440 | tf_op jit(solution)/shard_map/ppermute | solution.py:343
  36.8 0.0 collective-permute-start.5
  36.8 0.0 collective-permute-done.2.refs_2_
  36.8 1.6 %collective-permute-start.4 = (bf16[256,512]{1,0:T(8,128)(2,1)S(1)}, bf16[256,512]{1,0:T(8,128)(2,1)S(1)}, u32[]{:S(2)}, u32[]{:S(2)}) collective-permute-start(bf16[256,512]{1,0:T(8,128)(2,1)S(1)} %collective-permute-done.3.refs_0_), channel_id=1, source_target_pairs={{0,2},{1,3},{2,0},{3,1},{4,6},{5,7},{6,4},{7,5},{8,10},{9,11},{10,... | collective-permute-start | bytes 786440 | tf_op jit(solution)/shard_map/ppermute | solution.py:343
  38.4 0.0 collective-permute-done.1.refs_1_
  38.4 0.0 collective-permute-done.refs_0_
  38.4 2.2 %shard_map.155.before_ref = f32[256,512]{1,0:T(8,128)S(1)} custom-call(bf16[512,4096]{1,0:T(8,128)(2,1)} %weight_hbm.7, bf16[256,512]{1,0:T(8,128)(2,1)} %own_hbm.1, bf16[256,512]{1,0:T(8,128)(2,1)S(1)} %collective-permute-done.refs_0_, bf16[256,512]{1,0:T(8,128)(2,1)S(1)} %collective-permute-done.1.refs_1_, bf16[256,512]{1,0:T(8,128)(2,1)S(1)} %collective-permute-done.2.refs_2_), custom_call_target="tpu_custom_call" | custom-call | flops 1073741824 | bytes 4194304 | tf_op jit(solution)/shard_map/pallas_call | solution.py:313
  40.6 0.0 all-to-all-done.x_ref
  40.7 4.7 %shard_map.157 = (bf16[32,16,256]{2,1,0:T(8,128)(2,1)S(1)}, f32[2,16,64,256]{3,2,1,0:T(8,128)S(1)}) custom-call(bf16[32,2,16,256]{3,2,1,0:T(8,128)(2,1)S(1)} %all-to-all-done.x_ref, bf16[256,64]{1,0:T(8,128)(2,1)} %constant.10.clone.first_hbm, f32[4,64,128]{2,1,0:T(8,128)} %constant.14.clone.turns_hbm, bf16[2,256,256]{2,1,0:T(8,128)(2,1)} %constant.11.clone.over_hbm, ...), custom_call_target="tpu_custom_call" | custom-call | flops 2147483648 | bytes 4194304 | tf_op jit(solution)/shard_map/pallas_call | solution.py:313
  45.4 0.0 copy-start.2
  45.4 0.0 collective-permute-done.6.refs_3_
  45.4 0.5 collective-permute-done.5.refs_2_
  45.9 3.6 %collective-permute-done.4.refs_1_ = bf16[256,512]{1,0:T(8,128)(2,1)S(1)} collective-permute-done((bf16[256,512]{1,0:T(8,128)(2,1)S(1)}, bf16[256,512]{1,0:T(8,128)(2,1)S(1)}, u32[]{:S(2)}, u32[]{:S(2)}) %collective-permute-start.4) | collective-permute-done | bytes 262176 | tf_op jit(solution)/shard_map/ppermute | solution.py:343
  49.5 2.3 %shard_map.158 = (f32[256,512]{1,0:T(8,128)S(1)}, bf16[256,512]{1,0:T(8,128)(2,1)S(1)}, bf16[32,2,16,256]{3,2,1,0:T(8,128)(2,1)S(1)}) custom-call(bf16[512,4096]{1,0:T(8,128)(2,1)} %weight_hbm.7, bf16[256,512]{1,0:T(8,128)(2,1)} %queries_hbm.3, f32[256,512]{1,0:T(8,128)S(1)} %shard_map.155.before_ref, ...), custom_call_target="tpu_custom_call" | custom-call | flops 1073741824 | bytes 4194304 | tf_op jit(solution)/shard_map/pallas_call | solution.py:313
  51.8 29.3 %all_to_all.15.conv_ref.x_ref = bf16[32,2,16,256]{3,2,1,0:T(8,128)(2,1)S(1)} all-to-all(bf16[32,2,16,256]{3,2,1,0:T(8,128)(2,1)S(1)} %get-tuple-element.27), channel_id=1, replica_groups=mesh['seq'=32,'ch'=8] {'seq'}, dimensions={0} | all-to-all | bytes 1048576 | tf_op jit(solution)/shard_map/all_to_all | solution.py:317
  81.1 2.9 %shard_map.159 = (f32[256,512]{1,0:T(8,128)S(1)}, bf16[256,512]{1,0:T(8,128)(2,1)S(1)}, bf16[256,512]{1,0:T(8,128)(2,1)S(1)}, bf16[256,512]{1,0:T(8,128)(2,1)}, ...) custom-call(bf16[512,4096]{1,0:T(8,128)(2,1)} %weight_hbm.7, bf16[256,512]{1,0:T(8,128)(2,1)} %queries_hbm.3, ...), custom_call_target="tpu_custom_call" | custom-call | flops 1073741824 | bytes 4194304 | tf_op jit(solution)/shard_map/pallas_call | solution.py:313
  84.0 0.4 collective-permute-start.10
  84.4 0.3 collective-permute-start.11
  84.7 2.4 %collective-permute-start.12 = (bf16[256,512]{1,0:T(8,128)(2,1)S(1)}, bf16[256,512]{1,0:T(8,128)(2,1)}, u32[]{:S(2)}, u32[]{:S(2)}) collective-permute-start(bf16[256,512]{1,0:T(8,128)(2,1)S(1)} %get-tuple-element.37), channel_id=1, source_target_pairs={{0,3},{1,0},{2,1},{3,2},{4,7},{5,4},{6,5},{7,6},{8,11},{9,8},{10,9... | collective-permute-start | bytes 786440 | tf_op jit(solution)/shard_map/ppermute | solution.py:343
  87.1 5.6 %shard_map.161 = bf16[32,2,16,256]{3,2,1,0:T(8,128)(2,1)} custom-call(bf16[32,2,16,256]{3,2,1,0:T(8,128)(2,1)S(1)} %all_to_all.15.conv_ref.x_ref, f32[2,16,64,256]{3,2,1,0:T(8,128)S(1)} %get-tuple-element.40.spec_ref, bf16[256,64]{1,0:T(8,128)(2,1)} %constant.10.clone.first_hbm, f32[4,64,128]{2,1,0:T(8,128)} %constant.14.clone.turns_hbm, ...), custom_call_target="tpu_custom_call" | custom-call | flops 2147483648 | bytes 4194304 | tf_op jit(solution)/shard_map/pallas_call | solution.py:313
  92.7 5.8 %all-to-all-start.2 = ((bf16[32,2,16,256]{3,2,1,0:T(8,128)(2,1)}), bf16[32,2,16,256]{3,2,1,0:T(8,128)(2,1)S(1)}, u32[]{:S(2)}, u32[]{:S(2)}) async-start(bf16[32,2,16,256]{3,2,1,0:T(8,128)(2,1)} %shard_map.161), calls=%async_computation.2 | async-start | bytes 1048576 | tf_op jit(solution)/shard_map/all_to_all | solution.py:317
  98.6 0.0 copy-start
  98.6 0.0 copy-start.1
  98.6 2.4 %shard_map.160 = (bf16[256,512]{1,0:T(8,128)(2,1)S(1)}, bf16[256,512]{1,0:T(8,128)(2,1)S(1)}, bf16[256,512]{1,0:T(8,128)(2,1)S(1)}, bf16[256,512]{1,0:T(8,128)(2,1)S(1)}) custom-call(bf16[512,4096]{1,0:T(8,128)(2,1)} %weight_hbm.7, bf16[256,512]{1,0:T(8,128)(2,1)S(1)} %get-tuple-element.29.gated_ref), custom_call_target="tpu_custom_call" | custom-call | flops 1073741824 | bytes 4194304 | tf_op jit(solution)/shard_map/pallas_call | solution.py:313
  101.0 1.6 %collective-permute-start.7 = (bf16[256,512]{1,0:T(8,128)(2,1)S(1)}, bf16[256,512]{1,0:T(8,128)(2,1)S(1)}, u32[]{:S(2)}, u32[]{:S(2)}) collective-permute-start(bf16[256,512]{1,0:T(8,128)(2,1)S(1)} %get-tuple-element.31), channel_id=1, source_target_pairs={{0,2},{1,3},{2,0},{3,1},{4,6},{5,7},{6,4},{7,5},{8,10},{9,11},{10,... | collective-permute-start | bytes 786440 | tf_op jit(solution)/shard_map/ppermute | solution.py:343
  102.5 0.0 collective-permute-start.8
  102.5 0.0 collective-permute-done.10
  102.5 2.7 %collective-permute-start.9 = (bf16[256,512]{1,0:T(8,128)(2,1)S(1)}, bf16[256,512]{1,0:T(8,128)(2,1)S(1)}, u32[]{:S(2)}, u32[]{:S(2)}) collective-permute-start(bf16[256,512]{1,0:T(8,128)(2,1)S(1)} %get-tuple-element.33), channel_id=1, source_target_pairs={{0,3},{1,0},{2,1},{3,2},{4,7},{5,4},{6,5},{7,6},{8,11},{9,8},{10,9... | collective-permute-start | bytes 786440 | tf_op jit(solution)/shard_map/ppermute | solution.py:343
  105.2 0.0 collective-permute-done.11
  105.2 0.0 collective-permute-done.12
  105.2 1.2 %add_convert_fusion.1 = bf16[256,512]{1,0:T(8,128)(2,1)S(1)} fusion(bf16[256,512]{1,0:T(8,128)(2,1)} %collective-permute-done.12, bf16[256,512]{1,0:T(8,128)(2,1)} %collective-permute-done.11, bf16[256,512]{1,0:T(8,128)(2,1)} %collective-permute-done.10, bf16[256,512]{1,0:T(8,128)(2,1)S(1)} %get-tuple-element.34), kind=kLoop, calls=%fused_computation.2 | loop fusion | flops 1048576 | bytes 1310720 | tf_op jit(solution)/shard_map/convert_element_type | solution.py:423
  106.4 0.4 collective-permute-start.13
  106.9 0.8 multiply_convert_fusion
  107.6 2.5 %collective-permute-done.7 = bf16[256,512]{1,0:T(8,128)(2,1)S(1)} collective-permute-done((bf16[256,512]{1,0:T(8,128)(2,1)S(1)}, bf16[256,512]{1,0:T(8,128)(2,1)S(1)}, u32[]{:S(2)}, u32[]{:S(2)}) %collective-permute-start.7) | collective-permute-done | bytes 262176 | tf_op jit(solution)/shard_map/ppermute | solution.py:343
  110.1 6.3 %collective-permute-done.8 = bf16[256,512]{1,0:T(8,128)(2,1)S(1)} collective-permute-done((bf16[256,512]{1,0:T(8,128)(2,1)S(1)}, bf16[256,512]{1,0:T(8,128)(2,1)S(1)}, u32[]{:S(2)}, u32[]{:S(2)}) %collective-permute-start.8) | collective-permute-done | bytes 262176 | tf_op jit(solution)/shard_map/ppermute | solution.py:343
  116.4 0.0 collective-permute-done.9
  116.4 0.7 collective-permute-done.13
  117.1 0.9 add_convert_fusion
  117.9 0.0 all-to-all-done.2.res_ref
  117.9 0.0 copy-done
  118.0 1.1 shard_map.162
  (2 shorter events, 0.0 us)
Async XLA Ops:
  2.7 37.9 %all-to-all-start = ((bf16[32,2,16,256]{3,2,1,0:T(8,128)(2,1)}), bf16[32,2,16,256]{3,2,1,0:T(8,128)(2,1)S(1)}, u32[]{:S(2)}, u32[]{:S(2)}) async-start(bf16[32,2,16,256]{3,2,1,0:T(8,128)(2,1)} %get-tuple-element.25), calls=%async_computation | async-start | bytes 1048576 | tf_op jit(solution)/shard_map/all_to_all | solution.py:317
  15.3 18.7 %collective-permute-start.3 = (bf16[256,512]{1,0:T(8,128)(2,1)}, bf16[256,512]{1,0:T(8,128)(2,1)S(1)}, u32[]{:S(2)}, u32[]{:S(2)}) collective-permute-start(bf16[256,512]{1,0:T(8,128)(2,1)} %own_hbm.1), channel_id=1, source_target_pairs={{0,4},{1,5},{2,6},{3,7},{4,0},{5,1},{6,2},{7,3},{8,12},{9,13},{10,... | collective-permute-start | bytes 786440 | tf_op jit(solution)/shard_map/ppermute | solution.py:343
  16.2 20.6 %collective-permute-start.2 = (bf16[256,512]{1,0:T(8,128)(2,1)}, bf16[256,512]{1,0:T(8,128)(2,1)S(1)}, u32[]{:S(2)}, u32[]{:S(2)}) collective-permute-start(bf16[256,512]{1,0:T(8,128)(2,1)} %own_hbm.1), channel_id=1, source_target_pairs={{0,3},{1,0},{2,1},{3,2},{4,7},{5,4},{6,5},{7,6},{8,11},{9,8},{10,9... | collective-permute-start | bytes 786440 | tf_op jit(solution)/shard_map/ppermute | solution.py:343
  18.9 19.5 %collective-permute-start.1 = (bf16[256,512]{1,0:T(8,128)(2,1)}, bf16[256,512]{1,0:T(8,128)(2,1)S(1)}, u32[]{:S(2)}, u32[]{:S(2)}) collective-permute-start(bf16[256,512]{1,0:T(8,128)(2,1)} %own_hbm.1), channel_id=1, source_target_pairs={{0,1},{1,2},{2,3},{3,0},{4,5},{5,6},{6,7},{7,4},{8,9},{9,10},{10,1... | collective-permute-start | bytes 786440 | tf_op jit(solution)/shard_map/ppermute | solution.py:343
  18.9 19.5 %collective-permute-start = (bf16[256,512]{1,0:T(8,128)(2,1)}, bf16[256,512]{1,0:T(8,128)(2,1)S(1)}, u32[]{:S(2)}, u32[]{:S(2)}) collective-permute-start(bf16[256,512]{1,0:T(8,128)(2,1)} %own_hbm.1), channel_id=1, source_target_pairs={{0,2},{1,3},{2,0},{3,1},{4,6},{5,7},{6,4},{7,5},{8,10},{9,11},{10,... | collective-permute-start | bytes 786440 | tf_op jit(solution)/shard_map/ppermute | solution.py:343
  34.0 11.4 %collective-permute-start.6 = (bf16[256,512]{1,0:T(8,128)(2,1)S(1)}, bf16[256,512]{1,0:T(8,128)(2,1)S(1)}, u32[]{:S(2)}, u32[]{:S(2)}) collective-permute-start(bf16[256,512]{1,0:T(8,128)(2,1)S(1)} %collective-permute-done.3.refs_0_), channel_id=1, source_target_pairs={{0,3},{1,0},{2,1},{3,2},{4,7},{5,4},{6,5},{7,6},{8,11},{9,8},{10,9... | collective-permute-start | bytes 786440 | tf_op jit(solution)/shard_map/ppermute | solution.py:343
  36.8 9.1 %collective-permute-start.5 = (bf16[256,512]{1,0:T(8,128)(2,1)S(1)}, bf16[256,512]{1,0:T(8,128)(2,1)S(1)}, u32[]{:S(2)}, u32[]{:S(2)}) collective-permute-start(bf16[256,512]{1,0:T(8,128)(2,1)S(1)} %collective-permute-done.3.refs_0_), channel_id=1, source_target_pairs={{0,1},{1,2},{2,3},{3,0},{4,5},{5,6},{6,7},{7,4},{8,9},{9,10},{10,1... | collective-permute-start | bytes 786440 | tf_op jit(solution)/shard_map/ppermute | solution.py:343
  36.8 12.7 %collective-permute-start.4 = (bf16[256,512]{1,0:T(8,128)(2,1)S(1)}, bf16[256,512]{1,0:T(8,128)(2,1)S(1)}, u32[]{:S(2)}, u32[]{:S(2)}) collective-permute-start(bf16[256,512]{1,0:T(8,128)(2,1)S(1)} %collective-permute-done.3.refs_0_), channel_id=1, source_target_pairs={{0,2},{1,3},{2,0},{3,1},{4,6},{5,7},{6,4},{7,5},{8,10},{9,11},{10,... | collective-permute-start | bytes 786440 | tf_op jit(solution)/shard_map/ppermute | solution.py:343
  45.4 35.7 %copy-start.2 = (f32[512]{0:T(512)S(1)}, f32[512]{0:T(512)}, u32[]{:S(2)}) copy-start(f32[512]{0:T(512)} %param.16) | copy-start | bytes 6148
  84.0 18.5 %collective-permute-start.10 = (bf16[256,512]{1,0:T(8,128)(2,1)}, bf16[256,512]{1,0:T(8,128)(2,1)}, u32[]{:S(2)}, u32[]{:S(2)}) collective-permute-start(bf16[256,512]{1,0:T(8,128)(2,1)} %get-tuple-element.35), channel_id=1, source_target_pairs={{0,2},{1,3},{2,0},{3,1},{4,6},{5,7},{6,4},{7,5},{8,10},{9,11},{10,... | collective-permute-start | bytes 786440 | tf_op jit(solution)/shard_map/ppermute | solution.py:343
  84.4 20.8 %collective-permute-start.11 = (bf16[256,512]{1,0:T(8,128)(2,1)}, bf16[256,512]{1,0:T(8,128)(2,1)}, u32[]{:S(2)}, u32[]{:S(2)}) collective-permute-start(bf16[256,512]{1,0:T(8,128)(2,1)} %get-tuple-element.36), channel_id=1, source_target_pairs={{0,1},{1,2},{2,3},{3,0},{4,5},{5,6},{6,7},{7,4},{8,9},{9,10},{10,1... | collective-permute-start | bytes 786440 | tf_op jit(solution)/shard_map/ppermute | solution.py:343
  84.7 20.5 %collective-permute-start.12 = (bf16[256,512]{1,0:T(8,128)(2,1)S(1)}, bf16[256,512]{1,0:T(8,128)(2,1)}, u32[]{:S(2)}, u32[]{:S(2)}) collective-permute-start(bf16[256,512]{1,0:T(8,128)(2,1)S(1)} %get-tuple-element.37), channel_id=1, source_target_pairs={{0,3},{1,0},{2,1},{3,2},{4,7},{5,4},{6,5},{7,6},{8,11},{9,8},{10,9... | collective-permute-start | bytes 786440 | tf_op jit(solution)/shard_map/ppermute | solution.py:343
  92.7 25.2 %all-to-all-start.2 = ((bf16[32,2,16,256]{3,2,1,0:T(8,128)(2,1)}), bf16[32,2,16,256]{3,2,1,0:T(8,128)(2,1)S(1)}, u32[]{:S(2)}, u32[]{:S(2)}) async-start(bf16[32,2,16,256]{3,2,1,0:T(8,128)(2,1)} %shard_map.161), calls=%async_computation.2 | async-start | bytes 1048576 | tf_op jit(solution)/shard_map/all_to_all | solution.py:317
  98.6 19.4 %copy-start = (bf16[256,512]{1,0:T(8,128)(2,1)S(1)}, bf16[256,512]{1,0:T(8,128)(2,1)}, u32[]{:S(2)}) copy-start(bf16[256,512]{1,0:T(8,128)(2,1)} %key_ref.1) | copy-start | bytes 786436
  98.6 19.4 %copy-start.1 = (bf16[256,512]{1,0:T(8,128)(2,1)S(1)}, bf16[256,512]{1,0:T(8,128)(2,1)}, u32[]{:S(2)}) copy-start(bf16[256,512]{1,0:T(8,128)(2,1)} %value_ref.1) | copy-start | bytes 786436
  101.0 9.1 %collective-permute-start.7 = (bf16[256,512]{1,0:T(8,128)(2,1)S(1)}, bf16[256,512]{1,0:T(8,128)(2,1)S(1)}, u32[]{:S(2)}, u32[]{:S(2)}) collective-permute-start(bf16[256,512]{1,0:T(8,128)(2,1)S(1)} %get-tuple-element.31), channel_id=1, source_target_pairs={{0,2},{1,3},{2,0},{3,1},{4,6},{5,7},{6,4},{7,5},{8,10},{9,11},{10,... | collective-permute-start | bytes 786440 | tf_op jit(solution)/shard_map/ppermute | solution.py:343
  102.5 13.9 %collective-permute-start.8 = (bf16[256,512]{1,0:T(8,128)(2,1)S(1)}, bf16[256,512]{1,0:T(8,128)(2,1)S(1)}, u32[]{:S(2)}, u32[]{:S(2)}) collective-permute-start(bf16[256,512]{1,0:T(8,128)(2,1)S(1)} %get-tuple-element.32), channel_id=1, source_target_pairs={{0,1},{1,2},{2,3},{3,0},{4,5},{5,6},{6,7},{7,4},{8,9},{9,10},{10,1... | collective-permute-start | bytes 786440 | tf_op jit(solution)/shard_map/ppermute | solution.py:343
  102.5 13.9 %collective-permute-start.9 = (bf16[256,512]{1,0:T(8,128)(2,1)S(1)}, bf16[256,512]{1,0:T(8,128)(2,1)S(1)}, u32[]{:S(2)}, u32[]{:S(2)}) collective-permute-start(bf16[256,512]{1,0:T(8,128)(2,1)S(1)} %get-tuple-element.33), channel_id=1, source_target_pairs={{0,3},{1,0},{2,1},{3,2},{4,7},{5,4},{6,5},{7,6},{8,11},{9,8},{10,9... | collective-permute-start | bytes 786440 | tf_op jit(solution)/shard_map/ppermute | solution.py:343
  106.4 10.6 %collective-permute-start.13 = (bf16[256,512]{1,0:T(8,128)(2,1)S(1)}, bf16[256,512]{1,0:T(8,128)(2,1)S(1)}, u32[]{:S(2)}, u32[]{:S(2)}) collective-permute-start(bf16[256,512]{1,0:T(8,128)(2,1)S(1)} %add_convert_fusion.1), channel_id=1, source_target_pairs={{0,4},{1,5},{2,6},{3,7},{4,0},{5,1},{6,2},{7,3},{8,12},{9,13},{10,... | collective-permute-start | bytes 786440 | tf_op jit(solution)/shard_map/ppermute | solution.py:343
where the time goes:
time: 120 us; the launch traced here: 119 us
  starting transfers between devices  35.7 us (30%)
  blocking collectives  29.3 us (24%)
  waiting for transfers between devices  27.1 us (23%)
  Pallas kernels  23.4 us (20%)
  other arithmetic  2.89 us (2%)
    all_to_all x1, blocking collectives, to_all(): return lax.all_to_all(x, axis, split_axis=0, concat_axis=0, tiled=True)  29.3 us
    ppermute x14, waiting for transfers between devices, move(): return lax.ppermute(x, 'ch', pairs)  27 us
    pallas_call x8, Pallas kernels, call(): kernel(*(stay(x, pltpu.HBM) if i in hbm else x for i, x in enumerate(oper...  23.4 us
    all_to_all x2, starting transfers between devices, to_all(): return lax.all_to_all(x, axis, split_axis=0, concat_axis=0, tiled=True)  18.4 us
    ppermute x14, starting transfers between devices, move(): return lax.ppermute(x, 'ch', pairs)  17.3 us
  transfers between devices with their start and end apart: 16, of which 6 were waited for; matrix products, arithmetic and copies ran while one was open for 2% of the time, Pallas kernels for 13%

commit v1 on v0

--- a/solution.py
+++ b/solution.py
@@ -43,8 +43,8 @@
     last_high, last_low = split(last)
     return (
         np.concatenate([first_high, first_low], 0),
-        np.stack(split(over)),
-        np.stack(split(under)),
+        over.astype(bf16),
+        under.astype(bf16),
         np.concatenate([last_high, last_low], 0),
         turns.astype(np.float32),
     )
@@ -52,11 +52,6 @@
 
 def dot(a, b):
     return lax.dot_general(a, b, (((1,), (0,)), ((), ())), preferred_element_type=f32)
-
-
-def halves(x):
-    high = x.astype(bf16)
-    return high, (x - high.astype(f32)).astype(bf16)
 
 
 def forward(x, first, turns):
@@ -70,17 +65,15 @@
 
 
 def lanes_dot(x, table):
-    high, low = halves(x)
-    return dot(high, table[0]) + dot(low, table[0]) + dot(high, table[1])
+    return dot(x.astype(bf16), table[...])
 
 
 def backward(b, last, turns):
     real, imag = b[:, :LANES], b[:, LANES:]
     d = jnp.concatenate([real * turns[2] - imag * turns[3], real * turns[3] + imag * turns[2]], 0)
-    high, low = halves(d)
     rows = last.shape[0] // 2
-    both = dot(last, high)
-    return both[:rows] + both[rows:] + dot(last[:rows], low)
+    both = dot(last, d.astype(bf16))
+    return both[:rows] + both[rows:]
 
 
 def product(a, b, conjugate):
@@ -136,67 +129,44 @@
 
 
 def conv_body(
-    x_ref, first_hbm, turns_hbm, over_hbm, under_hbm, last_hbm, out_ref, spec_ref,
-    a_ref, rows_ref, first_ref, turns_ref, over_ref, under_ref, last_ref, sems,
+    x_ref, first_ref, turns_ref, over_ref, under_hbm, last_hbm, weight_hbm, queries_hbm,
+    out_ref, spec_ref, weight_ref, queries_ref, a_ref, rows_ref, under_ref, last_ref, sems,
 ):
-    copies = fetch(
-        [
-            (first_hbm, first_ref),
-            (turns_hbm, turns_ref),
-            (over_hbm, over_ref),
-            (under_hbm, under_ref),
-            (last_hbm, last_ref),
-        ],
-        sems,
-    )
+    pairs = [(under_hbm, under_ref), (last_hbm, last_ref)]
+    pairs += weight_pairs(weight_hbm, weight_ref, 1) + [(queries_hbm, queries_ref)]
+    copies = fetch(pairs, sems)
     devices, _, width, _ = x_ref.shape
     half = turns_ref.shape[1]
     for s in range(2):
         spread(x_ref[:, s], rows_ref)
-        if s == 0:
-            copies[0].wait()
-            copies[1].wait()
         for c in range(width):
             x = channel(rows_ref, c, devices, width)
             a_ref[s, c] = forward(x, first_ref[...], turns_ref)
-    for copy in copies[2:]:
-        copy.wait()
     spectra = lanes_dot(a_ref[...].reshape(2 * width * half, 2 * LANES), over_ref)
     spec_ref[...] = spectra.reshape(spec_ref.shape)
     for c in range(width):
         a_ref[0, c] = product(spec_ref[1, c], spec_ref[0, c], False)
+    copies[0].wait()
+    copies[1].wait()
     b = lanes_dot(a_ref[0].reshape(width * half, 2 * LANES), under_ref)
     a_ref[1] = b.reshape(width, half, 2 * LANES)
     for c in range(width):
         y = backward(a_ref[1, c], last_ref[...], turns_ref)
         put_channel(rows_ref, c, devices, width, y)
     gather(rows_ref, out_ref, None)
+    for copy in copies[2:]:
+        copy.wait()
 
 
 def back_body(
-    x_ref, spec_ref, first_hbm, turns_hbm, over_hbm, under_hbm, last_hbm, out_ref,
-    a_ref, rows_ref, first_ref, turns_ref, over_ref, under_ref, last_ref, sems,
+    x_ref, spec_ref, first_ref, turns_ref, over_ref, under_ref, last_ref, out_ref, a_ref, rows_ref
 ):
-    copies = fetch(
-        [
-            (first_hbm, first_ref),
-            (turns_hbm, turns_ref),
-            (over_hbm, over_ref),
-            (under_hbm, under_ref),
-            (last_hbm, last_ref),
-        ],
-        sems,
-    )
     devices, _, width, _ = x_ref.shape
     half = turns_ref.shape[1]
     spread(x_ref[:, 1], rows_ref)
-    copies[0].wait()
-    copies[1].wait()
     for c in range(width):
         x = channel(rows_ref, c, devices, width)
         a_ref[0, c] = forward(x, first_ref[...], turns_ref)
-    for copy in copies[2:]:
-        copy.wait()
     g = lanes_dot(a_ref[0].reshape(width * half, 2 * LANES), over_ref)
     a_ref[0] = g.reshape(width, half, 2 * LANES)
     for c in range(width):
@@ -216,73 +186,80 @@
     return (index // near + flip) % 2 * near + (index % near + shift) % near
 
 
-def weight_pairs(weight_hbm, weight_ref, flip, signed_hops):
+def weight_pairs(weight_hbm, weight_ref, flip):
     here = lax.axis_index("ch")
-    near = len(signed_hops)
-    width = weight_ref.shape[2]
+    near, _, width = weight_ref.shape
     pairs = []
-    for k, d in enumerate(signed_hops):
-        start = pl.multiple_of(peer(here, near, flip, d + near) * width, width)
+    for k in range(near):
+        start = pl.multiple_of(peer(here, near, flip, k) * width, width)
         pairs.append((weight_hbm.at[:, pl.ds(start, width)], weight_ref.at[k]))
     return pairs
 
 
-def mixed_terms(copies, weight_ref, parts):
+def mixed_term(part_ref, block):
+    return lax.dot_general(
+        part_ref[...], block, (((1,), (1,)), ((), ())), preferred_element_type=f32
+    )
+
+
+def mixed_body(hops, weight_hbm, own_hbm, *refs):
+    near = len(hops)
+    others = (len(refs) - near - 3) // 2
+    parts = refs[: near - 1]
+    others_hbm = refs[near - 1 : near - 1 + others]
+    out_ref, *others_ref = refs[near - 1 + others : -3]
+    own_ref, weight_ref, sems = refs[-3:]
+    pairs = [(own_hbm, own_ref)] + weight_pairs(weight_hbm, weight_ref, 0)
+    copies = fetch(pairs + list(zip(others_hbm, others_ref)), sems)
+    for copy in copies[: 1 + near]:
+        copy.wait()
     total = None
-    for k, part in enumerate(parts):
-        copies[k].wait()
-        term = lax.dot_general(
-            part[...], weight_ref[k], (((1,), (1,)), ((), ())), preferred_element_type=f32
-        )
+    for part_ref, d in zip((own_ref, *parts), hops):
+        term = mixed_term(part_ref, weight_ref[-d % near])
         total = term if total is None else total + term
-    return total
-
-
-def mixed_body(hops, weight_hbm, own_hbm, *refs):
-    *parts, out_ref, own_ref, weight_ref, sems = refs
-    pairs = [(own_hbm, own_ref)] + weight_pairs(weight_hbm, weight_ref, 0, [-d for d in hops])
-    copies = fetch(pairs, sems)
-    copies[0].wait()
-    out_ref[...] = mixed_terms(copies[1:], weight_ref, [own_ref] + parts)
-
-
-def conv_grad_body(hops, weight_hbm, queries_hbm, before_ref, forward_ref, *refs):
-    *parts, mixed_ref, conv_ref, sent_ref, queries_ref, weight_ref, sems = refs
-    pairs = weight_pairs(weight_hbm, weight_ref, 1, [-d for d in hops])
-    copies = fetch(pairs + [(queries_hbm, queries_ref)], sems)
+    out_ref[...] = total
+    for copy in copies[1 + near :]:
+        copy.wait()
+
+
+def conv_grad_body(hops, weight_ref, queries_ref, before_ref, forward_ref, *refs):
+    near = len(hops)
+    others = (len(refs) - near - 4) // 2
+    parts = refs[:near]
+    others_hbm = refs[near : near + others]
+    mixed_ref, conv_ref, sent_ref, *others_ref = refs[near + others : -1]
+    copies = fetch(list(zip(others_hbm, others_ref)), refs[-1])
     sent_ref[:, 0] = forward_ref[...]
-    mixed = before_ref[...] + mixed_terms(copies, weight_ref, parts)
+    mixed = before_ref[...]
+    for part_ref, d in zip(parts, hops):
+        mixed = mixed + mixed_term(part_ref, weight_ref[-d % near])
     mixed_ref[...] = mixed
-    copies[-1].wait()
     g = (mixed * queries_ref[...].astype(f32)).astype(bf16)
     conv_ref[...] = g
     sent_ref[:, 1] = g.T.reshape(forward_ref.shape)
-
-
-def project(copies, weight_ref, gated, out_refs):
-    for k, out_ref in enumerate(out_refs):
-        copies[k].wait()
-        out_ref[...] = dot(gated, weight_ref[k]).astype(bf16)
-
-
-def gate_body(hops, weight_hbm, queries_hbm, conv_ref, pkv_ref, skip_ref, *refs):
-    convolved_ref, gated_ref, *out_refs, queries_ref, weight_ref, sems = refs
-    pairs = weight_pairs(weight_hbm, weight_ref, 1, hops)
-    copies = fetch([(queries_hbm, queries_ref)] + pairs, sems)
+    for copy in copies:
+        copy.wait()
+
+
+def gate_body(hops, weight_ref, queries_ref, conv_ref, pkv_ref, skip_ref, *refs):
+    convolved_ref, gated_ref, *out_refs = refs
     local_rows = queries_ref.shape[0]
     conv = conv_ref[:, 0].reshape(-1, local_rows).T.astype(f32)
     convolved = conv + skip_ref[...] * pkv_ref[...].astype(f32)
     convolved_ref[...] = convolved
-    copies[0].wait()
     gated = (queries_ref[...].astype(f32) * convolved).astype(bf16)
     gated_ref[...] = gated
-    project(copies[1:], weight_ref, gated, out_refs)
+    for out_ref, d in zip(out_refs, hops):
+        out_ref[...] = dot(gated, weight_ref[d]).astype(bf16)
 
 
 def project_body(hops, weight_hbm, gated_ref, *refs):
     *out_refs, weight_ref, sems = refs
-    copies = fetch(weight_pairs(weight_hbm, weight_ref, 0, hops), sems)
-    project(copies, weight_ref, gated_ref[...], out_refs)
+    copies = fetch(weight_pairs(weight_hbm, weight_ref, 0), sems)
+    for copy in copies:
+        copy.wait()
+    for out_ref, d in zip(out_refs, hops):
+        out_ref[...] = dot(gated_ref[...], weight_ref[d]).astype(bf16)
 
 
 def finish_body(res_ref, conv_ref, skip_ref, key_ref, value_ref, gk_ref, gv_ref, gf_ref):
@@ -334,9 +311,9 @@
     work = [
         pltpu.VMEM((2, width, half, 2 * LANES), f32),
         pltpu.VMEM((local_rows // LANES, seq_devices * width, LANES), f32),
-    ] + [pltpu.VMEM(t.shape, t.dtype) for t in table]
+    ]
     own = pltpu.VMEM(flat, bf16)
-    weights = pltpu.VMEM((near, local_width, local_width), bf16)
+    blocks = (near, local_width, local_width)
 
     def move(x, flip, shift):
         pairs = [(i, peer(i, near, flip, shift)) for i in range(ch_devices)]
@@ -359,50 +336,51 @@
     signals = to_all(sent, "seq")
     other_parts = [other] + [move(other, 0, d) for d in hops]
 
-    (mixed,) = call(
+    mixed, *first_table = call(
         body(mixed_body),
-        (out_weight, cotangent, *own_parts),
-        [(flat, f32)],
-        [own, weights],
+        (out_weight, cotangent, *own_parts, *table[:3]),
+        [(flat, f32)] + [(t.shape, t.dtype) for t in table[:3]],
+        [own, pltpu.VMEM(blocks, bf16)],
         1 << 30,
-        hbm=(0, 1),
-        copies=1 + near,
-    )
-    conv, spectra = call(
+        hbm=(0, 1, *range(1 + near, 4 + near)),
+        copies=4 + near,
+    )
+    conv, spectra, far_weight, own_queries = call(
         conv_body,
-        (signals, *table),
-        [(message, bf16), ((2, width, half, 2 * LANES), f32)],
-        work,
+        (signals, *first_table, *table[3:], out_weight, queries),
+        [
+            (message, bf16),
+            ((2, width, half, 2 * LANES), f32),
+            (blocks, bf16),
+            (flat, bf16),
+        ],
+        work + [pltpu.VMEM(t.shape, t.dtype) for t in table[3:]],
         1 << 31,
-        hbm=range(1, 6),
-        copies=5,
-    )
-    mixed, grad_conv, both = call(
+        hbm=(4, 5, 6, 7),
+        copies=near + 3,
+    )
+    mixed, grad_conv, both, *last_table = call(
         body(conv_grad_body),
-        (out_weight, queries, mixed, conv, *other_parts),
-        [(flat, f32), (flat, bf16), (pair, bf16)],
-        [own, weights],
-        1 << 30,
-        hbm=(0, 1),
-        copies=1 + near,
+        (far_weight, own_queries, mixed, conv, *other_parts, *table),
+        [(flat, f32), (flat, bf16), (pair, bf16)] + [(t.shape, t.dtype) for t in table],
+        flops=1 << 30,
+        hbm=range(4 + near, 4 + near + len(table)),
+        copies=len(table),
     )
     both = to_all(both, "seq")
 
     convolved, gated, *far_terms = call(
         body(gate_body),
-        (out_weight, queries, both, pkv, skip),
+        (far_weight, own_queries, both, pkv, skip),
         [(flat, f32), (flat, bf16)] + [(flat, bf16)] * near,
-        [own, weights],
-        1 << 30,
-        hbm=(0, 1),
-        copies=1 + near,
+        flops=1 << 30,
     )
     far_terms = far_terms[:1] + [move(x, 0, d) for x, d in zip(far_terms[1:], hops)]
     near_terms = call(
         body(project_body),
         (out_weight, gated),
         [(flat, bf16)] * near,
-        [weights],
+        [pltpu.VMEM(blocks, bf16)],
         1 << 30,
         hbm=(0,),
         copies=near,
@@ -410,12 +388,10 @@
     near_terms = near_terms[:1] + [move(x, 0, d) for x, d in zip(near_terms[1:], hops)]
     (results,) = call(
         back_body,
-        (both, spectra, *table),
+        (both, spectra, *last_table),
         [(pair, bf16)],
         work,
         1 << 31,
-        hbm=range(2, 7),
-        copies=5,
     )
     results = to_all(results, "seq")
 

time: 120 us -> 113 us (0.942)
  Pallas kernels: 23.4 us -> 15.5 us
  waiting for transfers between devices: 27.1 us -> 28.4 us
    pallas_call x8, Pallas kernels: 23.4 us -> 15.5 us  [call(): kernel(*(stay(x, pltpu.HBM) if i in hbm else x for i, x in enumerate(oper...]
    ppermute x14, waiting for transfers between devices: 27 us -> 28.4 us  [move(): return lax.ppermute(x, 'ch', pairs)]
  transfers between devices with their start and end apart: 16 -> 16, of which waited for: 6 -> 6; matrix products, arithmetic and copies ran while one was open for 2% -> 3% of each run, Pallas kernels for 13% -> 9%
where the time goes in v1:
time: 113 us
  starting transfers between devices  35.7 us (32%)
  blocking collectives  29.3 us (26%)
  waiting for transfers between devices  28.4 us (25%)
  Pallas kernels  15.5 us (14%)
  other arithmetic  2.94 us (3%)
    all_to_all x1, blocking collectives, to_all(): return lax.all_to_all(x, axis, split_axis=0, concat_axis=0, tiled=True)  29.3 us
    ppermute x14, waiting for transfers between devices, move(): return lax.ppermute(x, 'ch', pairs)  28.4 us
    all_to_all x2, starting transfers between devices, to_all(): return lax.all_to_all(x, axis, split_axis=0, concat_axis=0, tiled=True)  18.4 us
    ppermute x14, starting transfers between devices, move(): return lax.ppermute(x, 'ch', pairs)  17.3 us
    pallas_call x8, Pallas kernels, call(): kernel(*(stay(x, pltpu.HBM) if i in hbm else x for i, x in enumerate(oper...  15.5 us
  transfers between devices with their start and end apart: 16, of which 6 were waited for; matrix products, arithmetic and copies ran while one was open for 3% of the time, Pallas kernels for 9%

profile of v1, /device:TPU:1, one launch (start us, length us, event | category | flops | bytes accessed | tf_op | source)
XLA Modules:
  0.0 112.5 jit_solution(12480400115159134417)
XLA Ops:
  0.6 2.1 %shard_map.155 = (bf16[32,2,16,256]{3,2,1,0:T(8,128)(2,1)}, bf16[256,512]{1,0:T(8,128)(2,1)S(1)}) custom-call(bf16[256,512]{1,0:T(8,128)(2,1)} %key_ref.1, bf16[256,512]{1,0:T(8,128)(2,1)} %value_ref.1, bf16[256,512]{1,0:T(8,128)(2,1)} %filter_hbm.1), custom_call_target="tpu_custom_call" | custom-call | flops 1048576 | bytes 4194304 | tf_op jit(solution)/shard_map/pallas_call | solution.py:290
  2.8 12.6 %all-to-all-start = ((bf16[32,2,16,256]{3,2,1,0:T(8,128)(2,1)}), bf16[32,2,16,256]{3,2,1,0:T(8,128)(2,1)S(1)}, u32[]{:S(2)}, u32[]{:S(2)}) async-start(bf16[32,2,16,256]{3,2,1,0:T(8,128)(2,1)} %get-tuple-element.36), calls=%async_computation | async-start | bytes 1048576 | tf_op jit(solution)/shard_map/all_to_all | solution.py:294
  15.3 0.8 collective-permute-start.3
  16.2 2.7 %collective-permute-start.2 = (bf16[256,512]{1,0:T(8,128)(2,1)}, bf16[256,512]{1,0:T(8,128)(2,1)S(1)}, u32[]{:S(2)}, u32[]{:S(2)}) collective-permute-start(bf16[256,512]{1,0:T(8,128)(2,1)} %own_hbm.1), channel_id=1, source_target_pairs={{0,3},{1,0},{2,1},{3,2},{4,7},{5,4},{6,5},{7,6},{8,11},{9,8},{10,9... | collective-permute-start | bytes 786440 | tf_op jit(solution)/shard_map/ppermute | solution.py:320
  18.9 0.0 collective-permute-start.1
  18.9 1.6 %collective-permute-start = (bf16[256,512]{1,0:T(8,128)(2,1)}, bf16[256,512]{1,0:T(8,128)(2,1)S(1)}, u32[]{:S(2)}, u32[]{:S(2)}) collective-permute-start(bf16[256,512]{1,0:T(8,128)(2,1)} %own_hbm.1), channel_id=1, source_target_pairs={{0,2},{1,3},{2,0},{3,1},{4,6},{5,7},{6,4},{7,5},{8,10},{9,11},{10,... | collective-permute-start | bytes 786440 | tf_op jit(solution)/shard_map/ppermute | solution.py:320
  20.6 13.5 %collective-permute-done.3.refs_0_ = bf16[256,512]{1,0:T(8,128)(2,1)S(1)} collective-permute-done((bf16[256,512]{1,0:T(8,128)(2,1)}, bf16[256,512]{1,0:T(8,128)(2,1)S(1)}, u32[]{:S(2)}, u32[]{:S(2)}) %collective-permute-start.3) | collective-permute-done | bytes 262176 | tf_op jit(solution)/shard_map/ppermute | solution.py:320
  34.0 2.7 %collective-permute-start.6 = (bf16[256,512]{1,0:T(8,128)(2,1)S(1)}, bf16[256,512]{1,0:T(8,128)(2,1)S(1)}, u32[]{:S(2)}, u32[]{:S(2)}) collective-permute-start(bf16[256,512]{1,0:T(8,128)(2,1)S(1)} %collective-permute-done.3.refs_0_), channel_id=1, source_target_pairs={{0,3},{1,0},{2,1},{3,2},{4,7},{5,4},{6,5},{7,6},{8,11},{9,8},{10,9... | collective-permute-start | bytes 786440 | tf_op jit(solution)/shard_map/ppermute | solution.py:320
  36.8 0.0 collective-permute-start.5
  36.8 0.0 collective-permute-done.2.refs_2_
  36.8 1.6 %collective-permute-start.4 = (bf16[256,512]{1,0:T(8,128)(2,1)S(1)}, bf16[256,512]{1,0:T(8,128)(2,1)S(1)}, u32[]{:S(2)}, u32[]{:S(2)}) collective-permute-start(bf16[256,512]{1,0:T(8,128)(2,1)S(1)} %collective-permute-done.3.refs_0_), channel_id=1, source_target_pairs={{0,2},{1,3},{2,0},{3,1},{4,6},{5,7},{6,4},{7,5},{8,10},{9,11},{10,... | collective-permute-start | bytes 786440 | tf_op jit(solution)/shard_map/ppermute | solution.py:320
  38.4 0.0 collective-permute-done.1.refs_1_
  38.4 0.0 collective-permute-done.refs_0_
  38.4 2.4 %shard_map.156 = (f32[256,512]{1,0:T(8,128)S(1)}, bf16[256,64]{1,0:T(8,128)(2,1)S(1)}, f32[4,64,128]{2,1,0:T(8,128)S(1)}, bf16[256,256]{1,0:T(8,128)(2,1)S(1)}) custom-call(bf16[512,4096]{1,0:T(8,128)(2,1)} %weight_hbm.5, bf16[256,512]{1,0:T(8,128)(2,1)} %own_hbm.1, bf16[256,512]{1,0:T(8,128)(2,1)S(1)} %collective-permute-done.refs_0_, ...), custom_call_target="tpu_custom_call" | custom-call | flops 1073741824 | bytes 4194304 | tf_op jit(solution)/shard_map/pallas_call | solution.py:290
  40.8 0.0 all-to-all-done.x_ref
  40.9 2.8 %shard_map.157 = (bf16[32,16,256]{2,1,0:T(8,128)(2,1)S(1)}, f32[2,16,64,256]{3,2,1,0:T(8,128)S(1)}, bf16[4,512,512]{2,1,0:T(8,128)(2,1)S(1)}, bf16[256,512]{1,0:T(8,128)(2,1)S(1)}) custom-call(bf16[32,2,16,256]{3,2,1,0:T(8,128)(2,1)S(1)} %all-to-all-done.x_ref, bf16[256,64]{1,0:T(8,128)(2,1)S(1)} %get-tuple-element.37.first_ref, ...), custom_call_target="tpu_custom_call" | custom-call | flops 2147483648 | bytes 4194304 | tf_op jit(solution)/shard_map/pallas_call | solution.py:290
  43.7 0.0 collective-permute-done.6.refs_3_
  43.7 2.2 %collective-permute-done.5.refs_2_ = bf16[256,512]{1,0:T(8,128)(2,1)S(1)} collective-permute-done((bf16[256,512]{1,0:T(8,128)(2,1)S(1)}, bf16[256,512]{1,0:T(8,128)(2,1)S(1)}, u32[]{:S(2)}, u32[]{:S(2)}) %collective-permute-start.5) | collective-permute-done | bytes 262176 | tf_op jit(solution)/shard_map/ppermute | solution.py:320
  45.9 3.6 %collective-permute-done.4.refs_1_ = bf16[256,512]{1,0:T(8,128)(2,1)S(1)} collective-permute-done((bf16[256,512]{1,0:T(8,128)(2,1)S(1)}, bf16[256,512]{1,0:T(8,128)(2,1)S(1)}, u32[]{:S(2)}, u32[]{:S(2)}) %collective-permute-start.4) | collective-permute-done | bytes 262176 | tf_op jit(solution)/shard_map/ppermute | solution.py:320
  49.5 1.4 %shard_map.158 = (f32[256,512]{1,0:T(8,128)S(1)}, bf16[256,512]{1,0:T(8,128)(2,1)S(1)}, bf16[32,2,16,256]{3,2,1,0:T(8,128)(2,1)S(1)}, bf16[256,64]{1,0:T(8,128)(...) custom-call(bf16[4,512,512]{2,1,0:T(8,128)(2,1)S(1)} %get-tuple-elem, ...), custom_call_target="tpu_custom_call" | custom-call | flops 1073741824 | bytes 4194304 | tf_op jit(solution)/shard_map/pallas_call | solution.py:290
  50.9 29.3 %all_to_all.15.conv_ref.x_ref = bf16[32,2,16,256]{3,2,1,0:T(8,128)(2,1)S(1)} all-to-all(bf16[32,2,16,256]{3,2,1,0:T(8,128)(2,1)S(1)} %get-tuple-element.44), channel_id=1, replica_groups=mesh['seq'=32,'ch'=8] {'seq'}, dimensions={0} | all-to-all | bytes 1048576 | tf_op jit(solution)/shard_map/all_to_all | solution.py:294
  80.2 0.0 copy-done.2
  80.2 0.8 shard_map.159
  80.9 0.4 collective-permute-start.10
  81.3 0.3 collective-permute-start.11
  81.6 2.4 %collective-permute-start.12 = (bf16[256,512]{1,0:T(8,128)(2,1)S(1)}, bf16[256,512]{1,0:T(8,128)(2,1)}, u32[]{:S(2)}, u32[]{:S(2)}) collective-permute-start(bf16[256,512]{1,0:T(8,128)(2,1)S(1)} %get-tuple-element.54), channel_id=1, source_target_pairs={{0,3},{1,0},{2,1},{3,2},{4,7},{5,4},{6,5},{7,6},{8,11},{9,8},{10,9... | collective-permute-start | bytes 786440 | tf_op jit(solution)/shard_map/ppermute | solution.py:320
  84.0 2.5 %shard_map.161 = bf16[32,2,16,256]{3,2,1,0:T(8,128)(2,1)} custom-call(bf16[32,2,16,256]{3,2,1,0:T(8,128)(2,1)S(1)} %all_to_all.15.conv_ref.x_ref, f32[2,16,64,256]{3,2,1,0:T(8,128)S(1)} %get-tuple-element.57.spec_ref, bf16[256,64]{1,0:T(8,128)(2,1)S(1)} %get-tuple-element.58.first_ref, f32[4,64,128]{2,1,0:T(8,128)S(1)} %get-tuple-element.59.turns_ref, ...), custom_call_target="tpu_custom_call" | custom-call | flops 2147483648 | bytes 4194304 | tf_op jit(solution)/shard_map/pallas_call | solution.py:290
  86.5 5.8 %all-to-all-start.2 = ((bf16[32,2,16,256]{3,2,1,0:T(8,128)(2,1)}), bf16[32,2,16,256]{3,2,1,0:T(8,128)(2,1)S(1)}, u32[]{:S(2)}, u32[]{:S(2)}) async-start(bf16[32,2,16,256]{3,2,1,0:T(8,128)(2,1)} %shard_map.161), calls=%async_computation.2 | async-start | bytes 1048576 | tf_op jit(solution)/shard_map/all_to_all | solution.py:294
  92.4 2.3 %shard_map.160 = (bf16[256,512]{1,0:T(8,128)(2,1)S(1)}, bf16[256,512]{1,0:T(8,128)(2,1)S(1)}, bf16[256,512]{1,0:T(8,128)(2,1)S(1)}, bf16[256,512]{1,0:T(8,128)(2,1)S(1)}) custom-call(bf16[512,4096]{1,0:T(8,128)(2,1)} %weight_hbm.5, bf16[256,512]{1,0:T(8,128)(2,1)S(1)} %get-tuple-element.46.gated_ref), custom_call_target="tpu_custom_call" | custom-call | flops 1073741824 | bytes 4194304 | tf_op jit(solution)/shard_map/pallas_call | solution.py:290
  94.7 1.6 %collective-permute-start.7 = (bf16[256,512]{1,0:T(8,128)(2,1)S(1)}, bf16[256,512]{1,0:T(8,128)(2,1)S(1)}, u32[]{:S(2)}, u32[]{:S(2)}) collective-permute-start(bf16[256,512]{1,0:T(8,128)(2,1)S(1)} %get-tuple-element.48), channel_id=1, source_target_pairs={{0,2},{1,3},{2,0},{3,1},{4,6},{5,7},{6,4},{7,5},{8,10},{9,11},{10,... | collective-permute-start | bytes 786440 | tf_op jit(solution)/shard_map/ppermute | solution.py:320
  96.2 0.0 collective-permute-start.8
  96.2 0.0 collective-permute-done.10
  96.2 2.7 %collective-permute-start.9 = (bf16[256,512]{1,0:T(8,128)(2,1)S(1)}, bf16[256,512]{1,0:T(8,128)(2,1)S(1)}, u32[]{:S(2)}, u32[]{:S(2)}) collective-permute-start(bf16[256,512]{1,0:T(8,128)(2,1)S(1)} %get-tuple-element.50), channel_id=1, source_target_pairs={{0,3},{1,0},{2,1},{3,2},{4,7},{5,4},{6,5},{7,6},{8,11},{9,8},{10,9... | collective-permute-start | bytes 786440 | tf_op jit(solution)/shard_map/ppermute | solution.py:320
  98.9 0.0 collective-permute-done.11
  98.9 0.0 collective-permute-done.12
  98.9 0.0 copy-start.1
  98.9 1.3 %add_convert_fusion.1 = bf16[256,512]{1,0:T(8,128)(2,1)S(1)} fusion(bf16[256,512]{1,0:T(8,128)(2,1)} %collective-permute-done.12, bf16[256,512]{1,0:T(8,128)(2,1)} %collective-permute-done.11, bf16[256,512]{1,0:T(8,128)(2,1)} %collective-permute-done.10, bf16[256,512]{1,0:T(8,128)(2,1)S(1)} %get-tuple-element.51), kind=kLoop, calls=%fused_computation.2 | loop fusion | flops 1048576 | bytes 1310720 | tf_op jit(solution)/shard_map/convert_element_type | solution.py:399
  100.2 0.4 collective-permute-start.13
  100.7 0.8 multiply_convert_fusion
  101.4 2.4 %collective-permute-done.7 = bf16[256,512]{1,0:T(8,128)(2,1)S(1)} collective-permute-done((bf16[256,512]{1,0:T(8,128)(2,1)S(1)}, bf16[256,512]{1,0:T(8,128)(2,1)S(1)}, u32[]{:S(2)}, u32[]{:S(2)}) %collective-permute-start.7) | collective-permute-done | bytes 262176 | tf_op jit(solution)/shard_map/ppermute | solution.py:320
  103.8 6.3 %collective-permute-done.8 = bf16[256,512]{1,0:T(8,128)(2,1)S(1)} collective-permute-done((bf16[256,512]{1,0:T(8,128)(2,1)S(1)}, bf16[256,512]{1,0:T(8,128)(2,1)S(1)}, u32[]{:S(2)}, u32[]{:S(2)}) %collective-permute-start.8) | collective-permute-done | bytes 262176 | tf_op jit(solution)/shard_map/ppermute | solution.py:320
  110.1 0.0 collective-permute-done.9
  110.1 0.4 collective-permute-done.13
  110.5 0.9 add_convert_fusion
  111.4 0.0 all-to-all-done.2.res_ref
  111.4 0.0 copy-done
  111.4 0.0 copy-done.1
  111.4 1.1 %shard_map.162 = (bf16[256,512]{1,0:T(8,128)(2,1)}, bf16[256,512]{1,0:T(8,128)(2,1)}, bf16[256,512]{1,0:T(8,128)(2,1)}) custom-call(bf16[32,2,16,256]{3,2,1,0:T(8,128)(2,1)S(1)} %all-to-all-done.2.res_ref, bf16[256,512]{1,0:T(8,128)(2,1)S(1)} %get-tuple-element.63.conv_ref, f32[1,512]{1,0:T(1,128)S(1)} %bitcast.2, bf16[256,512]{1,0:T(8,128)(2,1)S(1)} %copy-done, ...), custom_call_target="tpu_custom_call" | custom-call | flops 1048576 | bytes 4194304 | tf_op jit(solution)/shard_map/pallas_call | solution.py:290
  (2 shorter events, 0.0 us)
Async XLA Ops:
  2.8 38.1 %all-to-all-start = ((bf16[32,2,16,256]{3,2,1,0:T(8,128)(2,1)}), bf16[32,2,16,256]{3,2,1,0:T(8,128)(2,1)S(1)}, u32[]{:S(2)}, u32[]{:S(2)}) async-start(bf16[32,2,16,256]{3,2,1,0:T(8,128)(2,1)} %get-tuple-element.36), calls=%async_computation | async-start | bytes 1048576 | tf_op jit(solution)/shard_map/all_to_all | solution.py:294
  15.3 18.7 %collective-permute-start.3 = (bf16[256,512]{1,0:T(8,128)(2,1)}, bf16[256,512]{1,0:T(8,128)(2,1)S(1)}, u32[]{:S(2)}, u32[]{:S(2)}) collective-permute-start(bf16[256,512]{1,0:T(8,128)(2,1)} %own_hbm.1), channel_id=1, source_target_pairs={{0,4},{1,5},{2,6},{3,7},{4,0},{5,1},{6,2},{7,3},{8,12},{9,13},{10,... | collective-permute-start | bytes 786440 | tf_op jit(solution)/shard_map/ppermute | solution.py:320
  16.2 20.6 %collective-permute-start.2 = (bf16[256,512]{1,0:T(8,128)(2,1)}, bf16[256,512]{1,0:T(8,128)(2,1)S(1)}, u32[]{:S(2)}, u32[]{:S(2)}) collective-permute-start(bf16[256,512]{1,0:T(8,128)(2,1)} %own_hbm.1), channel_id=1, source_target_pairs={{0,3},{1,0},{2,1},{3,2},{4,7},{5,4},{6,5},{7,6},{8,11},{9,8},{10,9... | collective-permute-start | bytes 786440 | tf_op jit(solution)/shard_map/ppermute | solution.py:320
  18.9 19.5 %collective-permute-start.1 = (bf16[256,512]{1,0:T(8,128)(2,1)}, bf16[256,512]{1,0:T(8,128)(2,1)S(1)}, u32[]{:S(2)}, u32[]{:S(2)}) collective-permute-start(bf16[256,512]{1,0:T(8,128)(2,1)} %own_hbm.1), channel_id=1, source_target_pairs={{0,1},{1,2},{2,3},{3,0},{4,5},{5,6},{6,7},{7,4},{8,9},{9,10},{10,1... | collective-permute-start | bytes 786440 | tf_op jit(solution)/shard_map/ppermute | solution.py:320
  18.9 19.5 %collective-permute-start = (bf16[256,512]{1,0:T(8,128)(2,1)}, bf16[256,512]{1,0:T(8,128)(2,1)S(1)}, u32[]{:S(2)}, u32[]{:S(2)}) collective-permute-start(bf16[256,512]{1,0:T(8,128)(2,1)} %own_hbm.1), channel_id=1, source_target_pairs={{0,2},{1,3},{2,0},{3,1},{4,6},{5,7},{6,4},{7,5},{8,10},{9,11},{10,... | collective-permute-start | bytes 786440 | tf_op jit(solution)/shard_map/ppermute | solution.py:320
  34.0 9.7 %collective-permute-start.6 = (bf16[256,512]{1,0:T(8,128)(2,1)S(1)}, bf16[256,512]{1,0:T(8,128)(2,1)S(1)}, u32[]{:S(2)}, u32[]{:S(2)}) collective-permute-start(bf16[256,512]{1,0:T(8,128)(2,1)S(1)} %collective-permute-done.3.refs_0_), channel_id=1, source_target_pairs={{0,3},{1,0},{2,1},{3,2},{4,7},{5,4},{6,5},{7,6},{8,11},{9,8},{10,9... | collective-permute-start | bytes 786440 | tf_op jit(solution)/shard_map/ppermute | solution.py:320
  36.8 9.1 %collective-permute-start.5 = (bf16[256,512]{1,0:T(8,128)(2,1)S(1)}, bf16[256,512]{1,0:T(8,128)(2,1)S(1)}, u32[]{:S(2)}, u32[]{:S(2)}) collective-permute-start(bf16[256,512]{1,0:T(8,128)(2,1)S(1)} %collective-permute-done.3.refs_0_), channel_id=1, source_target_pairs={{0,1},{1,2},{2,3},{3,0},{4,5},{5,6},{6,7},{7,4},{8,9},{9,10},{10,1... | collective-permute-start | bytes 786440 | tf_op jit(solution)/shard_map/ppermute | solution.py:320
  36.8 12.7 %collective-permute-start.4 = (bf16[256,512]{1,0:T(8,128)(2,1)S(1)}, bf16[256,512]{1,0:T(8,128)(2,1)S(1)}, u32[]{:S(2)}, u32[]{:S(2)}) collective-permute-start(bf16[256,512]{1,0:T(8,128)(2,1)S(1)} %collective-permute-done.3.refs_0_), channel_id=1, source_target_pairs={{0,2},{1,3},{2,0},{3,1},{4,6},{5,7},{6,4},{7,5},{8,10},{9,11},{10,... | collective-permute-start | bytes 786440 | tf_op jit(solution)/shard_map/ppermute | solution.py:320
  49.5 30.7 %copy-start.2 = (f32[512]{0:T(512)S(1)}, f32[512]{0:T(512)}, u32[]{:S(2)}) copy-start(f32[512]{0:T(512)} %param.16) | copy-start | bytes 6148
  80.9 15.3 %collective-permute-start.10 = (bf16[256,512]{1,0:T(8,128)(2,1)S(1)}, bf16[256,512]{1,0:T(8,128)(2,1)}, u32[]{:S(2)}, u32[]{:S(2)}) collective-permute-start(bf16[256,512]{1,0:T(8,128)(2,1)S(1)} %get-tuple-element.52), channel_id=1, source_target_pairs={{0,2},{1,3},{2,0},{3,1},{4,6},{5,7},{6,4},{7,5},{8,10},{9,11},{10,... | collective-permute-start | bytes 786440 | tf_op jit(solution)/shard_map/ppermute | solution.py:320
  81.3 17.6 %collective-permute-start.11 = (bf16[256,512]{1,0:T(8,128)(2,1)S(1)}, bf16[256,512]{1,0:T(8,128)(2,1)}, u32[]{:S(2)}, u32[]{:S(2)}) collective-permute-start(bf16[256,512]{1,0:T(8,128)(2,1)S(1)} %get-tuple-element.53), channel_id=1, source_target_pairs={{0,1},{1,2},{2,3},{3,0},{4,5},{5,6},{6,7},{7,4},{8,9},{9,10},{10,1... | collective-permute-start | bytes 786440 | tf_op jit(solution)/shard_map/ppermute | solution.py:320
  81.6 17.3 %collective-permute-start.12 = (bf16[256,512]{1,0:T(8,128)(2,1)S(1)}, bf16[256,512]{1,0:T(8,128)(2,1)}, u32[]{:S(2)}, u32[]{:S(2)}) collective-permute-start(bf16[256,512]{1,0:T(8,128)(2,1)S(1)} %get-tuple-element.54), channel_id=1, source_target_pairs={{0,3},{1,0},{2,1},{3,2},{4,7},{5,4},{6,5},{7,6},{8,11},{9,8},{10,9... | collective-permute-start | bytes 786440 | tf_op jit(solution)/shard_map/ppermute | solution.py:320
  86.5 24.9 %all-to-all-start.2 = ((bf16[32,2,16,256]{3,2,1,0:T(8,128)(2,1)}), bf16[32,2,16,256]{3,2,1,0:T(8,128)(2,1)S(1)}, u32[]{:S(2)}, u32[]{:S(2)}) async-start(bf16[32,2,16,256]{3,2,1,0:T(8,128)(2,1)} %shard_map.161), calls=%async_computation.2 | async-start | bytes 1048576 | tf_op jit(solution)/shard_map/all_to_all | solution.py:294
  94.7 9.1 %collective-permute-start.7 = (bf16[256,512]{1,0:T(8,128)(2,1)S(1)}, bf16[256,512]{1,0:T(8,128)(2,1)S(1)}, u32[]{:S(2)}, u32[]{:S(2)}) collective-permute-start(bf16[256,512]{1,0:T(8,128)(2,1)S(1)} %get-tuple-element.48), channel_id=1, source_target_pairs={{0,2},{1,3},{2,0},{3,1},{4,6},{5,7},{6,4},{7,5},{8,10},{9,11},{10,... | collective-permute-start | bytes 786440 | tf_op jit(solution)/shard_map/ppermute | solution.py:320
  96.2 13.9 %collective-permute-start.8 = (bf16[256,512]{1,0:T(8,128)(2,1)S(1)}, bf16[256,512]{1,0:T(8,128)(2,1)S(1)}, u32[]{:S(2)}, u32[]{:S(2)}) collective-permute-start(bf16[256,512]{1,0:T(8,128)(2,1)S(1)} %get-tuple-element.49), channel_id=1, source_target_pairs={{0,1},{1,2},{2,3},{3,0},{4,5},{5,6},{6,7},{7,4},{8,9},{9,10},{10,1... | collective-permute-start | bytes 786440 | tf_op jit(solution)/shard_map/ppermute | solution.py:320
  96.2 13.9 %collective-permute-start.9 = (bf16[256,512]{1,0:T(8,128)(2,1)S(1)}, bf16[256,512]{1,0:T(8,128)(2,1)S(1)}, u32[]{:S(2)}, u32[]{:S(2)}) collective-permute-start(bf16[256,512]{1,0:T(8,128)(2,1)S(1)} %get-tuple-element.50), channel_id=1, source_target_pairs={{0,3},{1,0},{2,1},{3,2},{4,7},{5,4},{6,5},{7,6},{8,11},{9,8},{10,9... | collective-permute-start | bytes 786440 | tf_op jit(solution)/shard_map/ppermute | solution.py:320
  98.9 12.5 %copy-start = (bf16[256,512]{1,0:T(8,128)(2,1)S(1)}, bf16[256,512]{1,0:T(8,128)(2,1)}, u32[]{:S(2)}) copy-start(bf16[256,512]{1,0:T(8,128)(2,1)} %key_ref.1) | copy-start | bytes 786436
  98.9 12.5 %copy-start.1 = (bf16[256,512]{1,0:T(8,128)(2,1)S(1)}, bf16[256,512]{1,0:T(8,128)(2,1)}, u32[]{:S(2)}) copy-start(bf16[256,512]{1,0:T(8,128)(2,1)} %value_ref.1) | copy-start | bytes 786436
  100.2 10.3 %collective-permute-start.13 = (bf16[256,512]{1,0:T(8,128)(2,1)S(1)}, bf16[256,512]{1,0:T(8,128)(2,1)S(1)}, u32[]{:S(2)}, u32[]{:S(2)}) collective-permute-start(bf16[256,512]{1,0:T(8,128)(2,1)S(1)} %add_convert_fusion.1), channel_id=1, source_target_pairs={{0,4},{1,5},{2,6},{3,7},{4,0},{5,1},{6,2},{7,3},{8,12},{9,13},{10,... | collective-permute-start | bytes 786440 | tf_op jit(solution)/shard_map/ppermute | solution.py:320

commit v2 on v1

--- a/solution.py
+++ b/solution.py
@@ -54,26 +54,33 @@
     return lax.dot_general(a, b, (((1,), (0,)), ((), ())), preferred_element_type=f32)
 
 
-def forward(x, first, turns):
+def forward(signals, first, turns):
     half = turns.shape[1]
-    both = dot(first, x)
+    both = dot(first, jnp.concatenate(signals, 1))
     a = both[: 2 * half] + both[2 * half :]
-    real, imag = a[:half], a[half:]
-    return jnp.concatenate(
-        [real * turns[0] - imag * turns[1], real * turns[1] + imag * turns[0]], 1
-    )
+    rotated = []
+    for k in range(len(signals)):
+        real = a[:half, k * LANES : (k + 1) * LANES]
+        imag = a[half:, k * LANES : (k + 1) * LANES]
+        pair = [real * turns[0] - imag * turns[1], real * turns[1] + imag * turns[0]]
+        rotated.append(jnp.concatenate(pair, 1))
+    return rotated
 
 
 def lanes_dot(x, table):
     return dot(x.astype(bf16), table[...])
 
 
-def backward(b, last, turns):
-    real, imag = b[:, :LANES], b[:, LANES:]
-    d = jnp.concatenate([real * turns[2] - imag * turns[3], real * turns[3] + imag * turns[2]], 0)
+def backward(spectra, last, turns):
+    turned = []
+    for b in spectra:
+        real, imag = b[:, :LANES], b[:, LANES:]
+        pair = [real * turns[2] - imag * turns[3], real * turns[3] + imag * turns[2]]
+        turned.append(jnp.concatenate(pair, 0).astype(bf16))
     rows = last.shape[0] // 2
-    both = dot(last, d.astype(bf16))
-    return both[:rows] + both[rows:]
+    both = dot(last, jnp.concatenate(turned, 1))
+    y = both[:rows] + both[rows:]
+    return [y[:, k * LANES : (k + 1) * LANES] for k in range(len(spectra))]
 
 
 def product(a, b, conjugate):
@@ -139,9 +146,9 @@
     half = turns_ref.shape[1]
     for s in range(2):
         spread(x_ref[:, s], rows_ref)
-        for c in range(width):
-            x = channel(rows_ref, c, devices, width)
-            a_ref[s, c] = forward(x, first_ref[...], turns_ref)
+        for c in range(0, width, 2):
+            x = [channel(rows_ref, c + k, devices, width) for k in range(2)]
+            a_ref[s, c], a_ref[s, c + 1] = forward(x, first_ref[...], turns_ref)
     spectra = lanes_dot(a_ref[...].reshape(2 * width * half, 2 * LANES), over_ref)
     spec_ref[...] = spectra.reshape(spec_ref.shape)
     for c in range(width):
@@ -150,9 +157,10 @@
     copies[1].wait()
     b = lanes_dot(a_ref[0].reshape(width * half, 2 * LANES), under_ref)
     a_ref[1] = b.reshape(width, half, 2 * LANES)
-    for c in range(width):
-        y = backward(a_ref[1, c], last_ref[...], turns_ref)
-        put_channel(rows_ref, c, devices, width, y)
+    for c in range(0, width, 2):
+        y = backward([a_ref[1, c], a_ref[1, c + 1]], last_ref[...], turns_ref)
+        for k in range(2):
+            put_channel(rows_ref, c + k, devices, width, y[k])
     gather(rows_ref, out_ref, None)
     for copy in copies[2:]:
         copy.wait()
@@ -164,9 +172,9 @@
     devices, _, width, _ = x_ref.shape
     half = turns_ref.shape[1]
     spread(x_ref[:, 1], rows_ref)
-    for c in range(width):
-        x = channel(rows_ref, c, devices, width)
-        a_ref[0, c] = forward(x, first_ref[...], turns_ref)
+    for c in range(0, width, 2):
+        x = [channel(rows_ref, c + k, devices, width) for k in range(2)]
+        a_ref[0, c], a_ref[0, c + 1] = forward(x, first_ref[...], turns_ref)
     g = lanes_dot(a_ref[0].reshape(width * half, 2 * LANES), over_ref)
     a_ref[0] = g.reshape(width, half, 2 * LANES)
     for c in range(width):
@@ -176,9 +184,10 @@
     b = lanes_dot(a_ref[...].reshape(2 * width * half, 2 * LANES), under_ref)
     a_ref[...] = b.reshape(a_ref.shape)
     for s in range(2):
-        for c in range(width):
-            y = backward(a_ref[s, c], last_ref[...], turns_ref)
-            put_channel(rows_ref, c, devices, width, y)
+        for c in range(0, width, 2):
+            y = backward([a_ref[s, c], a_ref[s, c + 1]], last_ref[...], turns_ref)
+            for k in range(2):
+                put_channel(rows_ref, c + k, devices, width, y[k])
         gather(rows_ref, out_ref, s)
 
 
@@ -367,6 +376,13 @@
         hbm=range(4 + near, 4 + near + len(table)),
         copies=len(table),
     )
+
+    def moved(terms):
+        out = []
+        for k, d in enumerate(hops):
+            out.append(move(terms[1 + k], 0, d))
+        return out
+
     both = to_all(both, "seq")
 
     convolved, gated, *far_terms = call(
@@ -375,7 +391,7 @@
         [(flat, f32), (flat, bf16)] + [(flat, bf16)] * near,
         flops=1 << 30,
     )
-    far_terms = far_terms[:1] + [move(x, 0, d) for x, d in zip(far_terms[1:], hops)]
+    far_terms = far_terms[:1] + moved(far_terms)
     near_terms = call(
         body(project_body),
         (out_weight, gated),
@@ -385,7 +401,7 @@
         hbm=(0,),
         copies=near,
     )
-    near_terms = near_terms[:1] + [move(x, 0, d) for x, d in zip(near_terms[1:], hops)]
+    near_terms = near_terms[:1] + moved(near_terms)
     (results,) = call(
         back_body,
         (both, spectra, *last_table),

time: 113 us -> 113 us (level)
  no operation moved by 1% of the time
where the time goes in v2:
time: 113 us; the launch traced here: 112 us
  starting transfers between devices  35.7 us (32%)
  blocking collectives  29.3 us (26%)
  waiting for transfers between devices  28.5 us (25%)
  Pallas kernels  15.1 us (13%)
  other arithmetic  2.94 us (3%)
    all_to_all x1, blocking collectives, to_all(): return lax.all_to_all(x, axis, split_axis=0, concat_axis=0, tiled=True)  29.3 us
    ppermute x14, waiting for transfers between devices, move(): return lax.ppermute(x, 'ch', pairs)  28.5 us
    all_to_all x2, starting transfers between devices, to_all(): return lax.all_to_all(x, axis, split_axis=0, concat_axis=0, tiled=True)  18.4 us
    ppermute x14, starting transfers between devices, move(): return lax.ppermute(x, 'ch', pairs)  17.3 us
    pallas_call x8, Pallas kernels, call(): kernel(*(stay(x, pltpu.HBM) if i in hbm else x for i, x in enumerate(oper...  15.1 us
  transfers between devices with their start and end apart: 16, of which 6 were waited for; matrix products, arithmetic and copies ran while one was open for 3% of the time, Pallas kernels for 9%

profile of v2, /device:TPU:1, one launch (start us, length us, event | category | flops | bytes accessed | tf_op | source)
XLA Modules:
  0.0 112.3 jit_solution(7252218617925981548)
XLA Ops:
  0.6 2.1 %shard_map.155 = (bf16[32,2,16,256]{3,2,1,0:T(8,128)(2,1)}, bf16[256,512]{1,0:T(8,128)(2,1)S(1)}) custom-call(bf16[256,512]{1,0:T(8,128)(2,1)} %key_ref.1, bf16[256,512]{1,0:T(8,128)(2,1)} %value_ref.1, bf16[256,512]{1,0:T(8,128)(2,1)} %filter_hbm.1), custom_call_target="tpu_custom_call" | custom-call | flops 1048576 | bytes 4194304 | tf_op jit(solution)/shard_map/pallas_call | solution.py:299
  2.8 12.6 %all-to-all-start = ((bf16[32,2,16,256]{3,2,1,0:T(8,128)(2,1)}), bf16[32,2,16,256]{3,2,1,0:T(8,128)(2,1)S(1)}, u32[]{:S(2)}, u32[]{:S(2)}) async-start(bf16[32,2,16,256]{3,2,1,0:T(8,128)(2,1)} %get-tuple-element.36), calls=%async_computation | async-start | bytes 1048576 | tf_op jit(solution)/shard_map/all_to_all | solution.py:303
  15.3 0.8 collective-permute-start.3
  16.2 2.7 %collective-permute-start.2 = (bf16[256,512]{1,0:T(8,128)(2,1)}, bf16[256,512]{1,0:T(8,128)(2,1)S(1)}, u32[]{:S(2)}, u32[]{:S(2)}) collective-permute-start(bf16[256,512]{1,0:T(8,128)(2,1)} %own_hbm.1), channel_id=1, source_target_pairs={{0,3},{1,0},{2,1},{3,2},{4,7},{5,4},{6,5},{7,6},{8,11},{9,8},{10,9... | collective-permute-start | bytes 786440 | tf_op jit(solution)/shard_map/ppermute | solution.py:329
  18.9 0.0 collective-permute-start.1
  18.9 1.6 %collective-permute-start = (bf16[256,512]{1,0:T(8,128)(2,1)}, bf16[256,512]{1,0:T(8,128)(2,1)S(1)}, u32[]{:S(2)}, u32[]{:S(2)}) collective-permute-start(bf16[256,512]{1,0:T(8,128)(2,1)} %own_hbm.1), channel_id=1, source_target_pairs={{0,2},{1,3},{2,0},{3,1},{4,6},{5,7},{6,4},{7,5},{8,10},{9,11},{10,... | collective-permute-start | bytes 786440 | tf_op jit(solution)/shard_map/ppermute | solution.py:329
  20.6 13.5 %collective-permute-done.3.refs_0_ = bf16[256,512]{1,0:T(8,128)(2,1)S(1)} collective-permute-done((bf16[256,512]{1,0:T(8,128)(2,1)}, bf16[256,512]{1,0:T(8,128)(2,1)S(1)}, u32[]{:S(2)}, u32[]{:S(2)}) %collective-permute-start.3) | collective-permute-done | bytes 262176 | tf_op jit(solution)/shard_map/ppermute | solution.py:329
  34.0 2.7 %collective-permute-start.6 = (bf16[256,512]{1,0:T(8,128)(2,1)S(1)}, bf16[256,512]{1,0:T(8,128)(2,1)S(1)}, u32[]{:S(2)}, u32[]{:S(2)}) collective-permute-start(bf16[256,512]{1,0:T(8,128)(2,1)S(1)} %collective-permute-done.3.refs_0_), channel_id=1, source_target_pairs={{0,3},{1,0},{2,1},{3,2},{4,7},{5,4},{6,5},{7,6},{8,11},{9,8},{10,9... | collective-permute-start | bytes 786440 | tf_op jit(solution)/shard_map/ppermute | solution.py:329
  36.8 0.0 collective-permute-start.5
  36.8 0.0 collective-permute-done.2.refs_2_
  36.8 1.6 %collective-permute-start.4 = (bf16[256,512]{1,0:T(8,128)(2,1)S(1)}, bf16[256,512]{1,0:T(8,128)(2,1)S(1)}, u32[]{:S(2)}, u32[]{:S(2)}) collective-permute-start(bf16[256,512]{1,0:T(8,128)(2,1)S(1)} %collective-permute-done.3.refs_0_), channel_id=1, source_target_pairs={{0,2},{1,3},{2,0},{3,1},{4,6},{5,7},{6,4},{7,5},{8,10},{9,11},{10,... | collective-permute-start | bytes 786440 | tf_op jit(solution)/shard_map/ppermute | solution.py:329
  38.4 0.0 collective-permute-done.1.refs_1_
  38.4 0.0 collective-permute-done.refs_0_
  38.4 2.4 %shard_map.156 = (f32[256,512]{1,0:T(8,128)S(1)}, bf16[256,64]{1,0:T(8,128)(2,1)S(1)}, f32[4,64,128]{2,1,0:T(8,128)S(1)}, bf16[256,256]{1,0:T(8,128)(2,1)S(1)}) custom-call(bf16[512,4096]{1,0:T(8,128)(2,1)} %weight_hbm.5, bf16[256,512]{1,0:T(8,128)(2,1)} %own_hbm.1, bf16[256,512]{1,0:T(8,128)(2,1)S(1)} %collective-permute-done.refs_0_, ...), custom_call_target="tpu_custom_call" | custom-call | flops 1073741824 | bytes 4194304 | tf_op jit(solution)/shard_map/pallas_call | solution.py:299
  40.8 0.0 all-to-all-done.x_ref
  40.9 2.7 %shard_map.157 = (bf16[32,16,256]{2,1,0:T(8,128)(2,1)S(1)}, f32[2,16,64,256]{3,2,1,0:T(8,128)S(1)}, bf16[4,512,512]{2,1,0:T(8,128)(2,1)S(1)}, bf16[256,512]{1,0:T(8,128)(2,1)S(1)}) custom-call(bf16[32,2,16,256]{3,2,1,0:T(8,128)(2,1)S(1)} %all-to-all-done.x_ref, bf16[256,64]{1,0:T(8,128)(2,1)S(1)} %get-tuple-element.37.first_ref, ...), custom_call_target="tpu_custom_call" | custom-call | flops 2147483648 | bytes 4194304 | tf_op jit(solution)/shard_map/pallas_call | solution.py:299
  43.5 0.0 collective-permute-done.6.refs_3_
  43.6 2.3 %collective-permute-done.5.refs_2_ = bf16[256,512]{1,0:T(8,128)(2,1)S(1)} collective-permute-done((bf16[256,512]{1,0:T(8,128)(2,1)S(1)}, bf16[256,512]{1,0:T(8,128)(2,1)S(1)}, u32[]{:S(2)}, u32[]{:S(2)}) %collective-permute-start.5) | collective-permute-done | bytes 262176 | tf_op jit(solution)/shard_map/ppermute | solution.py:329
  45.9 3.6 %collective-permute-done.4.refs_1_ = bf16[256,512]{1,0:T(8,128)(2,1)S(1)} collective-permute-done((bf16[256,512]{1,0:T(8,128)(2,1)S(1)}, bf16[256,512]{1,0:T(8,128)(2,1)S(1)}, u32[]{:S(2)}, u32[]{:S(2)}) %collective-permute-start.4) | collective-permute-done | bytes 262176 | tf_op jit(solution)/shard_map/ppermute | solution.py:329
  49.5 1.4 %shard_map.158 = (f32[256,512]{1,0:T(8,128)S(1)}, bf16[256,512]{1,0:T(8,128)(2,1)S(1)}, bf16[32,2,16,256]{3,2,1,0:T(8,128)(2,1)S(1)}, bf16[256,64]{1,0:T(8,128)(...) custom-call(bf16[4,512,512]{2,1,0:T(8,128)(2,1)S(1)} %get-tuple-elem, ...), custom_call_target="tpu_custom_call" | custom-call | flops 1073741824 | bytes 4194304 | tf_op jit(solution)/shard_map/pallas_call | solution.py:299
  50.9 29.3 %all_to_all.15.conv_ref.x_ref = bf16[32,2,16,256]{3,2,1,0:T(8,128)(2,1)S(1)} all-to-all(bf16[32,2,16,256]{3,2,1,0:T(8,128)(2,1)S(1)} %get-tuple-element.44), channel_id=1, replica_groups=mesh['seq'=32,'ch'=8] {'seq'}, dimensions={0} | all-to-all | bytes 1048576 | tf_op jit(solution)/shard_map/all_to_all | solution.py:303
  80.2 0.0 copy-done.2
  80.2 0.8 shard_map.159
  80.9 0.4 collective-permute-start.10
  81.3 0.3 collective-permute-start.11
  81.6 2.4 %collective-permute-start.12 = (bf16[256,512]{1,0:T(8,128)(2,1)S(1)}, bf16[256,512]{1,0:T(8,128)(2,1)}, u32[]{:S(2)}, u32[]{:S(2)}) collective-permute-start(bf16[256,512]{1,0:T(8,128)(2,1)S(1)} %get-tuple-element.54), channel_id=1, source_target_pairs={{0,3},{1,0},{2,1},{3,2},{4,7},{5,4},{6,5},{7,6},{8,11},{9,8},{10,9... | collective-permute-start | bytes 786440 | tf_op jit(solution)/shard_map/ppermute | solution.py:329
  84.0 2.3 %shard_map.161 = bf16[32,2,16,256]{3,2,1,0:T(8,128)(2,1)} custom-call(bf16[32,2,16,256]{3,2,1,0:T(8,128)(2,1)S(1)} %all_to_all.15.conv_ref.x_ref, f32[2,16,64,256]{3,2,1,0:T(8,128)S(1)} %get-tuple-element.57.spec_ref, bf16[256,64]{1,0:T(8,128)(2,1)S(1)} %get-tuple-element.58.first_ref, f32[4,64,128]{2,1,0:T(8,128)S(1)} %get-tuple-element.59.turns_ref, ...), custom_call_target="tpu_custom_call" | custom-call | flops 2147483648 | bytes 4194304 | tf_op jit(solution)/shard_map/pallas_call | solution.py:299
  86.3 5.8 %all-to-all-start.2 = ((bf16[32,2,16,256]{3,2,1,0:T(8,128)(2,1)}), bf16[32,2,16,256]{3,2,1,0:T(8,128)(2,1)S(1)}, u32[]{:S(2)}, u32[]{:S(2)}) async-start(bf16[32,2,16,256]{3,2,1,0:T(8,128)(2,1)} %shard_map.161), calls=%async_computation.2 | async-start | bytes 1048576 | tf_op jit(solution)/shard_map/all_to_all | solution.py:303
  92.2 2.3 %shard_map.160 = (bf16[256,512]{1,0:T(8,128)(2,1)S(1)}, bf16[256,512]{1,0:T(8,128)(2,1)S(1)}, bf16[256,512]{1,0:T(8,128)(2,1)S(1)}, bf16[256,512]{1,0:T(8,128)(2,1)S(1)}) custom-call(bf16[512,4096]{1,0:T(8,128)(2,1)} %weight_hbm.5, bf16[256,512]{1,0:T(8,128)(2,1)S(1)} %get-tuple-element.46.gated_ref), custom_call_target="tpu_custom_call" | custom-call | flops 1073741824 | bytes 4194304 | tf_op jit(solution)/shard_map/pallas_call | solution.py:299
  94.5 1.6 %collective-permute-start.7 = (bf16[256,512]{1,0:T(8,128)(2,1)S(1)}, bf16[256,512]{1,0:T(8,128)(2,1)S(1)}, u32[]{:S(2)}, u32[]{:S(2)}) collective-permute-start(bf16[256,512]{1,0:T(8,128)(2,1)S(1)} %get-tuple-element.48), channel_id=1, source_target_pairs={{0,2},{1,3},{2,0},{3,1},{4,6},{5,7},{6,4},{7,5},{8,10},{9,11},{10,... | collective-permute-start | bytes 786440 | tf_op jit(solution)/shard_map/ppermute | solution.py:329
  96.1 0.0 collective-permute-start.8
  96.1 0.0 collective-permute-done.10
  96.1 2.7 %collective-permute-start.9 = (bf16[256,512]{1,0:T(8,128)(2,1)S(1)}, bf16[256,512]{1,0:T(8,128)(2,1)S(1)}, u32[]{:S(2)}, u32[]{:S(2)}) collective-permute-start(bf16[256,512]{1,0:T(8,128)(2,1)S(1)} %get-tuple-element.50), channel_id=1, source_target_pairs={{0,3},{1,0},{2,1},{3,2},{4,7},{5,4},{6,5},{7,6},{8,11},{9,8},{10,9... | collective-permute-start | bytes 786440 | tf_op jit(solution)/shard_map/ppermute | solution.py:329
  98.7 0.0 collective-permute-done.11
  98.7 0.0 collective-permute-done.12
  98.7 0.0 copy-start.1
  98.8 1.3 %add_convert_fusion.1 = bf16[256,512]{1,0:T(8,128)(2,1)S(1)} fusion(bf16[256,512]{1,0:T(8,128)(2,1)} %collective-permute-done.12, bf16[256,512]{1,0:T(8,128)(2,1)} %collective-permute-done.11, bf16[256,512]{1,0:T(8,128)(2,1)} %collective-permute-done.10, bf16[256,512]{1,0:T(8,128)(2,1)S(1)} %get-tuple-element.51), kind=kLoop, calls=%fused_computation.2 | loop fusion | flops 1048576 | bytes 1310720 | tf_op jit(solution)/shard_map/convert_element_type | solution.py:415
  100.1 0.4 collective-permute-start.13
  100.5 0.8 multiply_convert_fusion
  101.2 2.4 %collective-permute-done.7 = bf16[256,512]{1,0:T(8,128)(2,1)S(1)} collective-permute-done((bf16[256,512]{1,0:T(8,128)(2,1)S(1)}, bf16[256,512]{1,0:T(8,128)(2,1)S(1)}, u32[]{:S(2)}, u32[]{:S(2)}) %collective-permute-start.7) | collective-permute-done | bytes 262176 | tf_op jit(solution)/shard_map/ppermute | solution.py:329
  103.6 6.3 %collective-permute-done.8 = bf16[256,512]{1,0:T(8,128)(2,1)S(1)} collective-permute-done((bf16[256,512]{1,0:T(8,128)(2,1)S(1)}, bf16[256,512]{1,0:T(8,128)(2,1)S(1)}, u32[]{:S(2)}, u32[]{:S(2)}) %collective-permute-start.8) | collective-permute-done | bytes 262176 | tf_op jit(solution)/shard_map/ppermute | solution.py:329
  109.9 0.0 collective-permute-done.9
  109.9 0.4 collective-permute-done.13
  110.3 0.9 add_convert_fusion
  111.2 0.0 all-to-all-done.2.res_ref
  111.2 0.0 copy-done
  111.2 0.0 copy-done.1
  111.2 1.1 %shard_map.162 = (bf16[256,512]{1,0:T(8,128)(2,1)}, bf16[256,512]{1,0:T(8,128)(2,1)}, bf16[256,512]{1,0:T(8,128)(2,1)}) custom-call(bf16[32,2,16,256]{3,2,1,0:T(8,128)(2,1)S(1)} %all-to-all-done.2.res_ref, bf16[256,512]{1,0:T(8,128)(2,1)S(1)} %get-tuple-element.63.conv_ref, f32[1,512]{1,0:T(1,128)S(1)} %bitcast.2, bf16[256,512]{1,0:T(8,128)(2,1)S(1)} %copy-done, ...), custom_call_target="tpu_custom_call" | custom-call | flops 1048576 | bytes 4194304 | tf_op jit(solution)/shard_map/pallas_call | solution.py:299
  (2 shorter events, 0.0 us)
Async XLA Ops:
  2.8 38.1 %all-to-all-start = ((bf16[32,2,16,256]{3,2,1,0:T(8,128)(2,1)}), bf16[32,2,16,256]{3,2,1,0:T(8,128)(2,1)S(1)}, u32[]{:S(2)}, u32[]{:S(2)}) async-start(bf16[32,2,16,256]{3,2,1,0:T(8,128)(2,1)} %get-tuple-element.36), calls=%async_computation | async-start | bytes 1048576 | tf_op jit(solution)/shard_map/all_to_all | solution.py:303
  15.3 18.7 %collective-permute-start.3 = (bf16[256,512]{1,0:T(8,128)(2,1)}, bf16[256,512]{1,0:T(8,128)(2,1)S(1)}, u32[]{:S(2)}, u32[]{:S(2)}) collective-permute-start(bf16[256,512]{1,0:T(8,128)(2,1)} %own_hbm.1), channel_id=1, source_target_pairs={{0,4},{1,5},{2,6},{3,7},{4,0},{5,1},{6,2},{7,3},{8,12},{9,13},{10,... | collective-permute-start | bytes 786440 | tf_op jit(solution)/shard_map/ppermute | solution.py:329
  16.2 20.6 %collective-permute-start.2 = (bf16[256,512]{1,0:T(8,128)(2,1)}, bf16[256,512]{1,0:T(8,128)(2,1)S(1)}, u32[]{:S(2)}, u32[]{:S(2)}) collective-permute-start(bf16[256,512]{1,0:T(8,128)(2,1)} %own_hbm.1), channel_id=1, source_target_pairs={{0,3},{1,0},{2,1},{3,2},{4,7},{5,4},{6,5},{7,6},{8,11},{9,8},{10,9... | collective-permute-start | bytes 786440 | tf_op jit(solution)/shard_map/ppermute | solution.py:329
  18.9 19.5 %collective-permute-start.1 = (bf16[256,512]{1,0:T(8,128)(2,1)}, bf16[256,512]{1,0:T(8,128)(2,1)S(1)}, u32[]{:S(2)}, u32[]{:S(2)}) collective-permute-start(bf16[256,512]{1,0:T(8,128)(2,1)} %own_hbm.1), channel_id=1, source_target_pairs={{0,1},{1,2},{2,3},{3,0},{4,5},{5,6},{6,7},{7,4},{8,9},{9,10},{10,1... | collective-permute-start | bytes 786440 | tf_op jit(solution)/shard_map/ppermute | solution.py:329
  18.9 19.5 %collective-permute-start = (bf16[256,512]{1,0:T(8,128)(2,1)}, bf16[256,512]{1,0:T(8,128)(2,1)S(1)}, u32[]{:S(2)}, u32[]{:S(2)}) collective-permute-start(bf16[256,512]{1,0:T(8,128)(2,1)} %own_hbm.1), channel_id=1, source_target_pairs={{0,2},{1,3},{2,0},{3,1},{4,6},{5,7},{6,4},{7,5},{8,10},{9,11},{10,... | collective-permute-start | bytes 786440 | tf_op jit(solution)/shard_map/ppermute | solution.py:329
  34.0 9.5 %collective-permute-start.6 = (bf16[256,512]{1,0:T(8,128)(2,1)S(1)}, bf16[256,512]{1,0:T(8,128)(2,1)S(1)}, u32[]{:S(2)}, u32[]{:S(2)}) collective-permute-start(bf16[256,512]{1,0:T(8,128)(2,1)S(1)} %collective-permute-done.3.refs_0_), channel_id=1, source_target_pairs={{0,3},{1,0},{2,1},{3,2},{4,7},{5,4},{6,5},{7,6},{8,11},{9,8},{10,9... | collective-permute-start | bytes 786440 | tf_op jit(solution)/shard_map/ppermute | solution.py:329
  36.8 9.1 %collective-permute-start.5 = (bf16[256,512]{1,0:T(8,128)(2,1)S(1)}, bf16[256,512]{1,0:T(8,128)(2,1)S(1)}, u32[]{:S(2)}, u32[]{:S(2)}) collective-permute-start(bf16[256,512]{1,0:T(8,128)(2,1)S(1)} %collective-permute-done.3.refs_0_), channel_id=1, source_target_pairs={{0,1},{1,2},{2,3},{3,0},{4,5},{5,6},{6,7},{7,4},{8,9},{9,10},{10,1... | collective-permute-start | bytes 786440 | tf_op jit(solution)/shard_map/ppermute | solution.py:329
  36.8 12.7 %collective-permute-start.4 = (bf16[256,512]{1,0:T(8,128)(2,1)S(1)}, bf16[256,512]{1,0:T(8,128)(2,1)S(1)}, u32[]{:S(2)}, u32[]{:S(2)}) collective-permute-start(bf16[256,512]{1,0:T(8,128)(2,1)S(1)} %collective-permute-done.3.refs_0_), channel_id=1, source_target_pairs={{0,2},{1,3},{2,0},{3,1},{4,6},{5,7},{6,4},{7,5},{8,10},{9,11},{10,... | collective-permute-start | bytes 786440 | tf_op jit(solution)/shard_map/ppermute | solution.py:329
  49.5 30.7 %copy-start.2 = (f32[512]{0:T(512)S(1)}, f32[512]{0:T(512)}, u32[]{:S(2)}) copy-start(f32[512]{0:T(512)} %param.16) | copy-start | bytes 6148
  80.9 15.1 %collective-permute-start.10 = (bf16[256,512]{1,0:T(8,128)(2,1)S(1)}, bf16[256,512]{1,0:T(8,128)(2,1)}, u32[]{:S(2)}, u32[]{:S(2)}) collective-permute-start(bf16[256,512]{1,0:T(8,128)(2,1)S(1)} %get-tuple-element.52), channel_id=1, source_target_pairs={{0,2},{1,3},{2,0},{3,1},{4,6},{5,7},{6,4},{7,5},{8,10},{9,11},{10,... | collective-permute-start | bytes 786440 | tf_op jit(solution)/shard_map/ppermute | solution.py:329
  81.3 17.4 %collective-permute-start.11 = (bf16[256,512]{1,0:T(8,128)(2,1)S(1)}, bf16[256,512]{1,0:T(8,128)(2,1)}, u32[]{:S(2)}, u32[]{:S(2)}) collective-permute-start(bf16[256,512]{1,0:T(8,128)(2,1)S(1)} %get-tuple-element.53), channel_id=1, source_target_pairs={{0,1},{1,2},{2,3},{3,0},{4,5},{5,6},{6,7},{7,4},{8,9},{9,10},{10,1... | collective-permute-start | bytes 786440 | tf_op jit(solution)/shard_map/ppermute | solution.py:329
  81.6 17.1 %collective-permute-start.12 = (bf16[256,512]{1,0:T(8,128)(2,1)S(1)}, bf16[256,512]{1,0:T(8,128)(2,1)}, u32[]{:S(2)}, u32[]{:S(2)}) collective-permute-start(bf16[256,512]{1,0:T(8,128)(2,1)S(1)} %get-tuple-element.54), channel_id=1, source_target_pairs={{0,3},{1,0},{2,1},{3,2},{4,7},{5,4},{6,5},{7,6},{8,11},{9,8},{10,9... | collective-permute-start | bytes 786440 | tf_op jit(solution)/shard_map/ppermute | solution.py:329
  86.3 24.9 %all-to-all-start.2 = ((bf16[32,2,16,256]{3,2,1,0:T(8,128)(2,1)}), bf16[32,2,16,256]{3,2,1,0:T(8,128)(2,1)S(1)}, u32[]{:S(2)}, u32[]{:S(2)}) async-start(bf16[32,2,16,256]{3,2,1,0:T(8,128)(2,1)} %shard_map.161), calls=%async_computation.2 | async-start | bytes 1048576 | tf_op jit(solution)/shard_map/all_to_all | solution.py:303
  94.5 9.1 %collective-permute-start.7 = (bf16[256,512]{1,0:T(8,128)(2,1)S(1)}, bf16[256,512]{1,0:T(8,128)(2,1)S(1)}, u32[]{:S(2)}, u32[]{:S(2)}) collective-permute-start(bf16[256,512]{1,0:T(8,128)(2,1)S(1)} %get-tuple-element.48), channel_id=1, source_target_pairs={{0,2},{1,3},{2,0},{3,1},{4,6},{5,7},{6,4},{7,5},{8,10},{9,11},{10,... | collective-permute-start | bytes 786440 | tf_op jit(solution)/shard_map/ppermute | solution.py:329
  96.1 13.9 %collective-permute-start.8 = (bf16[256,512]{1,0:T(8,128)(2,1)S(1)}, bf16[256,512]{1,0:T(8,128)(2,1)S(1)}, u32[]{:S(2)}, u32[]{:S(2)}) collective-permute-start(bf16[256,512]{1,0:T(8,128)(2,1)S(1)} %get-tuple-element.49), channel_id=1, source_target_pairs={{0,1},{1,2},{2,3},{3,0},{4,5},{5,6},{6,7},{7,4},{8,9},{9,10},{10,1... | collective-permute-start | bytes 786440 | tf_op jit(solution)/shard_map/ppermute | solution.py:329
  96.1 13.9 %collective-permute-start.9 = (bf16[256,512]{1,0:T(8,128)(2,1)S(1)}, bf16[256,512]{1,0:T(8,128)(2,1)S(1)}, u32[]{:S(2)}, u32[]{:S(2)}) collective-permute-start(bf16[256,512]{1,0:T(8,128)(2,1)S(1)} %get-tuple-element.50), channel_id=1, source_target_pairs={{0,3},{1,0},{2,1},{3,2},{4,7},{5,4},{6,5},{7,6},{8,11},{9,8},{10,9... | collective-permute-start | bytes 786440 | tf_op jit(solution)/shard_map/ppermute | solution.py:329
  98.7 12.5 %copy-start = (bf16[256,512]{1,0:T(8,128)(2,1)S(1)}, bf16[256,512]{1,0:T(8,128)(2,1)}, u32[]{:S(2)}) copy-start(bf16[256,512]{1,0:T(8,128)(2,1)} %key_ref.1) | copy-start | bytes 786436
  98.7 12.5 %copy-start.1 = (bf16[256,512]{1,0:T(8,128)(2,1)S(1)}, bf16[256,512]{1,0:T(8,128)(2,1)}, u32[]{:S(2)}) copy-start(bf16[256,512]{1,0:T(8,128)(2,1)} %value_ref.1) | copy-start | bytes 786436
  100.1 10.3 %collective-permute-start.13 = (bf16[256,512]{1,0:T(8,128)(2,1)S(1)}, bf16[256,512]{1,0:T(8,128)(2,1)S(1)}, u32[]{:S(2)}, u32[]{:S(2)}) collective-permute-start(bf16[256,512]{1,0:T(8,128)(2,1)S(1)} %add_convert_fusion.1), channel_id=1, source_target_pairs={{0,4},{1,5},{2,6},{3,7},{4,0},{5,1},{6,2},{7,3},{8,12},{9,13},{10,... | collective-permute-start | bytes 786440 | tf_op jit(solution)/shard_map/ppermute | solution.py:329

commit v3 on v2

--- a/solution.py
+++ b/solution.py
@@ -99,15 +99,15 @@
 
 
 def prepare_body(key_hbm, value_hbm, filter_hbm, out_ref, pkv_ref, key_ref, value_ref, filter_ref, sems):
-    copies = fetch([(key_hbm, key_ref), (value_hbm, value_ref), (filter_hbm, filter_ref)], sems)
+    copies = fetch([(filter_hbm, filter_ref), (key_hbm, key_ref), (value_hbm, value_ref)], sems)
     peers, _, width, local_rows = out_ref.shape
     copies[0].wait()
+    out_ref[:, 1] = filter_ref[...].T.reshape(peers, width, local_rows)
     copies[1].wait()
+    copies[2].wait()
     pkv = (key_ref[...].astype(f32) * value_ref[...].astype(f32)).astype(bf16)
     pkv_ref[...] = pkv
     out_ref[:, 0] = pkv.T.reshape(peers, width, local_rows)
-    copies[2].wait()
-    out_ref[:, 1] = filter_ref[...].T.reshape(peers, width, local_rows)
 
 
 def spread(x, rows_ref):
@@ -265,10 +265,9 @@
 def project_body(hops, weight_hbm, gated_ref, *refs):
     *out_refs, weight_ref, sems = refs
     copies = fetch(weight_pairs(weight_hbm, weight_ref, 0), sems)
-    for copy in copies:
-        copy.wait()
-    for out_ref, d in zip(out_refs, hops):
-        out_ref[...] = dot(gated_ref[...], weight_ref[d]).astype(bf16)
+    for d in range(len(hops)):
+        copies[d].wait()
+        out_refs[hops.index(d)][...] = dot(gated_ref[...], weight_ref[d]).astype(bf16)
 
 
 def finish_body(res_ref, conv_ref, skip_ref, key_ref, value_ref, gk_ref, gv_ref, gf_ref):

time: 113 us -> 113 us (level)
  no operation moved by 1% of the time
where the time goes in v3:
time: 113 us; the launch traced here: 112 us
  starting transfers between devices  35.7 us (32%)
  blocking collectives  29.3 us (26%)
  waiting for transfers between devices  28.5 us (25%)
  Pallas kernels  15.1 us (13%)
  other arithmetic  2.94 us (3%)
    all_to_all x1, blocking collectives, to_all(): return lax.all_to_all(x, axis, split_axis=0, concat_axis=0, tiled=True)  29.3 us
    ppermute x14, waiting for transfers between devices, move(): return lax.ppermute(x, 'ch', pairs)  28.5 us
    all_to_all x2, starting transfers between devices, to_all(): return lax.all_to_all(x, axis, split_axis=0, concat_axis=0, tiled=True)  18.4 us
    ppermute x14, starting transfers between devices, move(): return lax.ppermute(x, 'ch', pairs)  17.3 us
    pallas_call x8, Pallas kernels, call(): kernel(*(stay(x, pltpu.HBM) if i in hbm else x for i, x in enumerate(oper...  15.1 us
  transfers between devices with their start and end apart: 16, of which 6 were waited for; matrix products, arithmetic and copies ran while one was open for 3% of the time, Pallas kernels for 9%

profile of v3, /device:TPU:1, one launch (start us, length us, event | category | flops | bytes accessed | tf_op | source)
XLA Modules:
  0.0 112.3 jit_solution(5491673422124278628)
XLA Ops:
  0.6 2.1 %shard_map.155 = (bf16[32,2,16,256]{3,2,1,0:T(8,128)(2,1)}, bf16[256,512]{1,0:T(8,128)(2,1)S(1)}) custom-call(bf16[256,512]{1,0:T(8,128)(2,1)} %key_ref.1, bf16[256,512]{1,0:T(8,128)(2,1)} %value_ref.1, bf16[256,512]{1,0:T(8,128)(2,1)} %filter_hbm.1), custom_call_target="tpu_custom_call" | custom-call | flops 1048576 | bytes 4194304 | tf_op jit(solution)/shard_map/pallas_call | solution.py:298
  2.7 12.6 %all-to-all-start = ((bf16[32,2,16,256]{3,2,1,0:T(8,128)(2,1)}), bf16[32,2,16,256]{3,2,1,0:T(8,128)(2,1)S(1)}, u32[]{:S(2)}, u32[]{:S(2)}) async-start(bf16[32,2,16,256]{3,2,1,0:T(8,128)(2,1)} %get-tuple-element.36), calls=%async_computation | async-start | bytes 1048576 | tf_op jit(solution)/shard_map/all_to_all | solution.py:302
  15.3 0.8 collective-permute-start.3
  16.1 2.7 %collective-permute-start.2 = (bf16[256,512]{1,0:T(8,128)(2,1)}, bf16[256,512]{1,0:T(8,128)(2,1)S(1)}, u32[]{:S(2)}, u32[]{:S(2)}) collective-permute-start(bf16[256,512]{1,0:T(8,128)(2,1)} %own_hbm.1), channel_id=1, source_target_pairs={{0,3},{1,0},{2,1},{3,2},{4,7},{5,4},{6,5},{7,6},{8,11},{9,8},{10,9... | collective-permute-start | bytes 786440 | tf_op jit(solution)/shard_map/ppermute | solution.py:328
  18.9 0.0 collective-permute-start.1
  18.9 1.6 %collective-permute-start = (bf16[256,512]{1,0:T(8,128)(2,1)}, bf16[256,512]{1,0:T(8,128)(2,1)S(1)}, u32[]{:S(2)}, u32[]{:S(2)}) collective-permute-start(bf16[256,512]{1,0:T(8,128)(2,1)} %own_hbm.1), channel_id=1, source_target_pairs={{0,2},{1,3},{2,0},{3,1},{4,6},{5,7},{6,4},{7,5},{8,10},{9,11},{10,... | collective-permute-start | bytes 786440 | tf_op jit(solution)/shard_map/ppermute | solution.py:328
  20.5 13.5 %collective-permute-done.3.refs_0_ = bf16[256,512]{1,0:T(8,128)(2,1)S(1)} collective-permute-done((bf16[256,512]{1,0:T(8,128)(2,1)}, bf16[256,512]{1,0:T(8,128)(2,1)S(1)}, u32[]{:S(2)}, u32[]{:S(2)}) %collective-permute-start.3) | collective-permute-done | bytes 262176 | tf_op jit(solution)/shard_map/ppermute | solution.py:328
  34.0 2.7 %collective-permute-start.6 = (bf16[256,512]{1,0:T(8,128)(2,1)S(1)}, bf16[256,512]{1,0:T(8,128)(2,1)S(1)}, u32[]{:S(2)}, u32[]{:S(2)}) collective-permute-start(bf16[256,512]{1,0:T(8,128)(2,1)S(1)} %collective-permute-done.3.refs_0_), channel_id=1, source_target_pairs={{0,3},{1,0},{2,1},{3,2},{4,7},{5,4},{6,5},{7,6},{8,11},{9,8},{10,9... | collective-permute-start | bytes 786440 | tf_op jit(solution)/shard_map/ppermute | solution.py:328
  36.7 0.0 collective-permute-start.5
  36.7 0.0 collective-permute-done.2.refs_2_
  36.7 1.6 %collective-permute-start.4 = (bf16[256,512]{1,0:T(8,128)(2,1)S(1)}, bf16[256,512]{1,0:T(8,128)(2,1)S(1)}, u32[]{:S(2)}, u32[]{:S(2)}) collective-permute-start(bf16[256,512]{1,0:T(8,128)(2,1)S(1)} %collective-permute-done.3.refs_0_), channel_id=1, source_target_pairs={{0,2},{1,3},{2,0},{3,1},{4,6},{5,7},{6,4},{7,5},{8,10},{9,11},{10,... | collective-permute-start | bytes 786440 | tf_op jit(solution)/shard_map/ppermute | solution.py:328
  38.4 0.0 collective-permute-done.1.refs_1_
  38.4 0.0 collective-permute-done.refs_0_
  38.4 2.4 %shard_map.156 = (f32[256,512]{1,0:T(8,128)S(1)}, bf16[256,64]{1,0:T(8,128)(2,1)S(1)}, f32[4,64,128]{2,1,0:T(8,128)S(1)}, bf16[256,256]{1,0:T(8,128)(2,1)S(1)}) custom-call(bf16[512,4096]{1,0:T(8,128)(2,1)} %weight_hbm.5, bf16[256,512]{1,0:T(8,128)(2,1)} %own_hbm.1, bf16[256,512]{1,0:T(8,128)(2,1)S(1)} %collective-permute-done.refs_0_, ...), custom_call_target="tpu_custom_call" | custom-call | flops 1073741824 | bytes 4194304 | tf_op jit(solution)/shard_map/pallas_call | solution.py:298
  40.8 0.0 all-to-all-done.x_ref
  40.8 2.7 %shard_map.157 = (bf16[32,16,256]{2,1,0:T(8,128)(2,1)S(1)}, f32[2,16,64,256]{3,2,1,0:T(8,128)S(1)}, bf16[4,512,512]{2,1,0:T(8,128)(2,1)S(1)}, bf16[256,512]{1,0:T(8,128)(2,1)S(1)}) custom-call(bf16[32,2,16,256]{3,2,1,0:T(8,128)(2,1)S(1)} %all-to-all-done.x_ref, bf16[256,64]{1,0:T(8,128)(2,1)S(1)} %get-tuple-element.37.first_ref, ...), custom_call_target="tpu_custom_call" | custom-call | flops 2147483648 | bytes 4194304 | tf_op jit(solution)/shard_map/pallas_call | solution.py:298
  43.5 0.0 collective-permute-done.6.refs_3_
  43.5 2.3 %collective-permute-done.5.refs_2_ = bf16[256,512]{1,0:T(8,128)(2,1)S(1)} collective-permute-done((bf16[256,512]{1,0:T(8,128)(2,1)S(1)}, bf16[256,512]{1,0:T(8,128)(2,1)S(1)}, u32[]{:S(2)}, u32[]{:S(2)}) %collective-permute-start.5) | collective-permute-done | bytes 262176 | tf_op jit(solution)/shard_map/ppermute | solution.py:328
  45.9 3.6 %collective-permute-done.4.refs_1_ = bf16[256,512]{1,0:T(8,128)(2,1)S(1)} collective-permute-done((bf16[256,512]{1,0:T(8,128)(2,1)S(1)}, bf16[256,512]{1,0:T(8,128)(2,1)S(1)}, u32[]{:S(2)}, u32[]{:S(2)}) %collective-permute-start.4) | collective-permute-done | bytes 262176 | tf_op jit(solution)/shard_map/ppermute | solution.py:328
  49.5 1.4 %shard_map.158 = (f32[256,512]{1,0:T(8,128)S(1)}, bf16[256,512]{1,0:T(8,128)(2,1)S(1)}, bf16[32,2,16,256]{3,2,1,0:T(8,128)(2,1)S(1)}, bf16[256,64]{1,0:T(8,128)(...) custom-call(bf16[4,512,512]{2,1,0:T(8,128)(2,1)S(1)} %get-tuple-elem, ...), custom_call_target="tpu_custom_call" | custom-call | flops 1073741824 | bytes 4194304 | tf_op jit(solution)/shard_map/pallas_call | solution.py:298
  50.8 29.3 %all_to_all.15.conv_ref.x_ref = bf16[32,2,16,256]{3,2,1,0:T(8,128)(2,1)S(1)} all-to-all(bf16[32,2,16,256]{3,2,1,0:T(8,128)(2,1)S(1)} %get-tuple-element.44), channel_id=1, replica_groups=mesh['seq'=32,'ch'=8] {'seq'}, dimensions={0} | all-to-all | bytes 1048576 | tf_op jit(solution)/shard_map/all_to_all | solution.py:302
  80.1 0.0 copy-done.2
  80.1 0.8 shard_map.159
  80.9 0.4 collective-permute-start.10
  81.3 0.3 collective-permute-start.11
  81.6 2.4 %collective-permute-start.12 = (bf16[256,512]{1,0:T(8,128)(2,1)S(1)}, bf16[256,512]{1,0:T(8,128)(2,1)}, u32[]{:S(2)}, u32[]{:S(2)}) collective-permute-start(bf16[256,512]{1,0:T(8,128)(2,1)S(1)} %get-tuple-element.54), channel_id=1, source_target_pairs={{0,3},{1,0},{2,1},{3,2},{4,7},{5,4},{6,5},{7,6},{8,11},{9,8},{10,9... | collective-permute-start | bytes 786440 | tf_op jit(solution)/shard_map/ppermute | solution.py:328
  84.0 2.3 %shard_map.161 = bf16[32,2,16,256]{3,2,1,0:T(8,128)(2,1)} custom-call(bf16[32,2,16,256]{3,2,1,0:T(8,128)(2,1)S(1)} %all_to_all.15.conv_ref.x_ref, f32[2,16,64,256]{3,2,1,0:T(8,128)S(1)} %get-tuple-element.57.spec_ref, bf16[256,64]{1,0:T(8,128)(2,1)S(1)} %get-tuple-element.58.first_ref, f32[4,64,128]{2,1,0:T(8,128)S(1)} %get-tuple-element.59.turns_ref, ...), custom_call_target="tpu_custom_call" | custom-call | flops 2147483648 | bytes 4194304 | tf_op jit(solution)/shard_map/pallas_call | solution.py:298
  86.3 5.8 %all-to-all-start.2 = ((bf16[32,2,16,256]{3,2,1,0:T(8,128)(2,1)}), bf16[32,2,16,256]{3,2,1,0:T(8,128)(2,1)S(1)}, u32[]{:S(2)}, u32[]{:S(2)}) async-start(bf16[32,2,16,256]{3,2,1,0:T(8,128)(2,1)} %shard_map.161), calls=%async_computation.2 | async-start | bytes 1048576 | tf_op jit(solution)/shard_map/all_to_all | solution.py:302
  92.1 2.3 %shard_map.160 = (bf16[256,512]{1,0:T(8,128)(2,1)S(1)}, bf16[256,512]{1,0:T(8,128)(2,1)S(1)}, bf16[256,512]{1,0:T(8,128)(2,1)S(1)}, bf16[256,512]{1,0:T(8,128)(2,1)S(1)}) custom-call(bf16[512,4096]{1,0:T(8,128)(2,1)} %weight_hbm.5, bf16[256,512]{1,0:T(8,128)(2,1)S(1)} %get-tuple-element.46.gated_ref), custom_call_target="tpu_custom_call" | custom-call | flops 1073741824 | bytes 4194304 | tf_op jit(solution)/shard_map/pallas_call | solution.py:298
  94.5 1.6 %collective-permute-start.7 = (bf16[256,512]{1,0:T(8,128)(2,1)S(1)}, bf16[256,512]{1,0:T(8,128)(2,1)S(1)}, u32[]{:S(2)}, u32[]{:S(2)}) collective-permute-start(bf16[256,512]{1,0:T(8,128)(2,1)S(1)} %get-tuple-element.48), channel_id=1, source_target_pairs={{0,2},{1,3},{2,0},{3,1},{4,6},{5,7},{6,4},{7,5},{8,10},{9,11},{10,... | collective-permute-start | bytes 786440 | tf_op jit(solution)/shard_map/ppermute | solution.py:328
  96.0 0.0 collective-permute-start.8
  96.0 0.0 collective-permute-done.10
  96.0 2.7 %collective-permute-start.9 = (bf16[256,512]{1,0:T(8,128)(2,1)S(1)}, bf16[256,512]{1,0:T(8,128)(2,1)S(1)}, u32[]{:S(2)}, u32[]{:S(2)}) collective-permute-start(bf16[256,512]{1,0:T(8,128)(2,1)S(1)} %get-tuple-element.50), channel_id=1, source_target_pairs={{0,3},{1,0},{2,1},{3,2},{4,7},{5,4},{6,5},{7,6},{8,11},{9,8},{10,9... | collective-permute-start | bytes 786440 | tf_op jit(solution)/shard_map/ppermute | solution.py:328
  98.7 0.0 collective-permute-done.11
  98.7 0.0 collective-permute-done.12
  98.7 0.0 copy-start.1
  98.7 1.3 %add_convert_fusion.1 = bf16[256,512]{1,0:T(8,128)(2,1)S(1)} fusion(bf16[256,512]{1,0:T(8,128)(2,1)} %collective-permute-done.12, bf16[256,512]{1,0:T(8,128)(2,1)} %collective-permute-done.11, bf16[256,512]{1,0:T(8,128)(2,1)} %collective-permute-done.10, bf16[256,512]{1,0:T(8,128)(2,1)S(1)} %get-tuple-element.51), kind=kLoop, calls=%fused_computation.2 | loop fusion | flops 1048576 | bytes 1310720 | tf_op jit(solution)/shard_map/convert_element_type | solution.py:414
  100.0 0.4 collective-permute-start.13
  100.4 0.8 multiply_convert_fusion
  101.2 2.4 %collective-permute-done.7 = bf16[256,512]{1,0:T(8,128)(2,1)S(1)} collective-permute-done((bf16[256,512]{1,0:T(8,128)(2,1)S(1)}, bf16[256,512]{1,0:T(8,128)(2,1)S(1)}, u32[]{:S(2)}, u32[]{:S(2)}) %collective-permute-start.7) | collective-permute-done | bytes 262176 | tf_op jit(solution)/shard_map/ppermute | solution.py:328
  103.6 6.3 %collective-permute-done.8 = bf16[256,512]{1,0:T(8,128)(2,1)S(1)} collective-permute-done((bf16[256,512]{1,0:T(8,128)(2,1)S(1)}, bf16[256,512]{1,0:T(8,128)(2,1)S(1)}, u32[]{:S(2)}, u32[]{:S(2)}) %collective-permute-start.8) | collective-permute-done | bytes 262176 | tf_op jit(solution)/shard_map/ppermute | solution.py:328
  109.9 0.0 collective-permute-done.9
  109.9 0.4 collective-permute-done.13
  110.3 0.9 add_convert_fusion
  111.2 0.0 all-to-all-done.2.res_ref
  111.2 0.0 copy-done
  111.2 0.0 copy-done.1
  111.2 1.1 %shard_map.162 = (bf16[256,512]{1,0:T(8,128)(2,1)}, bf16[256,512]{1,0:T(8,128)(2,1)}, bf16[256,512]{1,0:T(8,128)(2,1)}) custom-call(bf16[32,2,16,256]{3,2,1,0:T(8,128)(2,1)S(1)} %all-to-all-done.2.res_ref, bf16[256,512]{1,0:T(8,128)(2,1)S(1)} %get-tuple-element.63.conv_ref, f32[1,512]{1,0:T(1,128)S(1)} %bitcast.2, bf16[256,512]{1,0:T(8,128)(2,1)S(1)} %copy-done, ...), custom_call_target="tpu_custom_call" | custom-call | flops 1048576 | bytes 4194304 | tf_op jit(solution)/shard_map/pallas_call | solution.py:298
  (2 shorter events, 0.0 us)
Async XLA Ops:
  2.7 38.1 %all-to-all-start = ((bf16[32,2,16,256]{3,2,1,0:T(8,128)(2,1)}), bf16[32,2,16,256]{3,2,1,0:T(8,128)(2,1)S(1)}, u32[]{:S(2)}, u32[]{:S(2)}) async-start(bf16[32,2,16,256]{3,2,1,0:T(8,128)(2,1)} %get-tuple-element.36), calls=%async_computation | async-start | bytes 1048576 | tf_op jit(solution)/shard_map/all_to_all | solution.py:302
  15.3 18.7 %collective-permute-start.3 = (bf16[256,512]{1,0:T(8,128)(2,1)}, bf16[256,512]{1,0:T(8,128)(2,1)S(1)}, u32[]{:S(2)}, u32[]{:S(2)}) collective-permute-start(bf16[256,512]{1,0:T(8,128)(2,1)} %own_hbm.1), channel_id=1, source_target_pairs={{0,4},{1,5},{2,6},{3,7},{4,0},{5,1},{6,2},{7,3},{8,12},{9,13},{10,... | collective-permute-start | bytes 786440 | tf_op jit(solution)/shard_map/ppermute | solution.py:328
  16.1 20.6 %collective-permute-start.2 = (bf16[256,512]{1,0:T(8,128)(2,1)}, bf16[256,512]{1,0:T(8,128)(2,1)S(1)}, u32[]{:S(2)}, u32[]{:S(2)}) collective-permute-start(bf16[256,512]{1,0:T(8,128)(2,1)} %own_hbm.1), channel_id=1, source_target_pairs={{0,3},{1,0},{2,1},{3,2},{4,7},{5,4},{6,5},{7,6},{8,11},{9,8},{10,9... | collective-permute-start | bytes 786440 | tf_op jit(solution)/shard_map/ppermute | solution.py:328
  18.9 19.5 %collective-permute-start.1 = (bf16[256,512]{1,0:T(8,128)(2,1)}, bf16[256,512]{1,0:T(8,128)(2,1)S(1)}, u32[]{:S(2)}, u32[]{:S(2)}) collective-permute-start(bf16[256,512]{1,0:T(8,128)(2,1)} %own_hbm.1), channel_id=1, source_target_pairs={{0,1},{1,2},{2,3},{3,0},{4,5},{5,6},{6,7},{7,4},{8,9},{9,10},{10,1... | collective-permute-start | bytes 786440 | tf_op jit(solution)/shard_map/ppermute | solution.py:328
  18.9 19.5 %collective-permute-start = (bf16[256,512]{1,0:T(8,128)(2,1)}, bf16[256,512]{1,0:T(8,128)(2,1)S(1)}, u32[]{:S(2)}, u32[]{:S(2)}) collective-permute-start(bf16[256,512]{1,0:T(8,128)(2,1)} %own_hbm.1), channel_id=1, source_target_pairs={{0,2},{1,3},{2,0},{3,1},{4,6},{5,7},{6,4},{7,5},{8,10},{9,11},{10,... | collective-permute-start | bytes 786440 | tf_op jit(solution)/shard_map/ppermute | solution.py:328
  34.0 9.5 %collective-permute-start.6 = (bf16[256,512]{1,0:T(8,128)(2,1)S(1)}, bf16[256,512]{1,0:T(8,128)(2,1)S(1)}, u32[]{:S(2)}, u32[]{:S(2)}) collective-permute-start(bf16[256,512]{1,0:T(8,128)(2,1)S(1)} %collective-permute-done.3.refs_0_), channel_id=1, source_target_pairs={{0,3},{1,0},{2,1},{3,2},{4,7},{5,4},{6,5},{7,6},{8,11},{9,8},{10,9... | collective-permute-start | bytes 786440 | tf_op jit(solution)/shard_map/ppermute | solution.py:328
  36.7 9.1 %collective-permute-start.5 = (bf16[256,512]{1,0:T(8,128)(2,1)S(1)}, bf16[256,512]{1,0:T(8,128)(2,1)S(1)}, u32[]{:S(2)}, u32[]{:S(2)}) collective-permute-start(bf16[256,512]{1,0:T(8,128)(2,1)S(1)} %collective-permute-done.3.refs_0_), channel_id=1, source_target_pairs={{0,1},{1,2},{2,3},{3,0},{4,5},{5,6},{6,7},{7,4},{8,9},{9,10},{10,1... | collective-permute-start | bytes 786440 | tf_op jit(solution)/shard_map/ppermute | solution.py:328
  36.7 12.7 %collective-permute-start.4 = (bf16[256,512]{1,0:T(8,128)(2,1)S(1)}, bf16[256,512]{1,0:T(8,128)(2,1)S(1)}, u32[]{:S(2)}, u32[]{:S(2)}) collective-permute-start(bf16[256,512]{1,0:T(8,128)(2,1)S(1)} %collective-permute-done.3.refs_0_), channel_id=1, source_target_pairs={{0,2},{1,3},{2,0},{3,1},{4,6},{5,7},{6,4},{7,5},{8,10},{9,11},{10,... | collective-permute-start | bytes 786440 | tf_op jit(solution)/shard_map/ppermute | solution.py:328
  49.5 30.7 %copy-start.2 = (f32[512]{0:T(512)S(1)}, f32[512]{0:T(512)}, u32[]{:S(2)}) copy-start(f32[512]{0:T(512)} %param.16) | copy-start | bytes 6148
  80.9 15.1 %collective-permute-start.10 = (bf16[256,512]{1,0:T(8,128)(2,1)S(1)}, bf16[256,512]{1,0:T(8,128)(2,1)}, u32[]{:S(2)}, u32[]{:S(2)}) collective-permute-start(bf16[256,512]{1,0:T(8,128)(2,1)S(1)} %get-tuple-element.52), channel_id=1, source_target_pairs={{0,2},{1,3},{2,0},{3,1},{4,6},{5,7},{6,4},{7,5},{8,10},{9,11},{10,... | collective-permute-start | bytes 786440 | tf_op jit(solution)/shard_map/ppermute | solution.py:328
  81.3 17.4 %collective-permute-start.11 = (bf16[256,512]{1,0:T(8,128)(2,1)S(1)}, bf16[256,512]{1,0:T(8,128)(2,1)}, u32[]{:S(2)}, u32[]{:S(2)}) collective-permute-start(bf16[256,512]{1,0:T(8,128)(2,1)S(1)} %get-tuple-element.53), channel_id=1, source_target_pairs={{0,1},{1,2},{2,3},{3,0},{4,5},{5,6},{6,7},{7,4},{8,9},{9,10},{10,1... | collective-permute-start | bytes 786440 | tf_op jit(solution)/shard_map/ppermute | solution.py:328
  81.6 17.1 %collective-permute-start.12 = (bf16[256,512]{1,0:T(8,128)(2,1)S(1)}, bf16[256,512]{1,0:T(8,128)(2,1)}, u32[]{:S(2)}, u32[]{:S(2)}) collective-permute-start(bf16[256,512]{1,0:T(8,128)(2,1)S(1)} %get-tuple-element.54), channel_id=1, source_target_pairs={{0,3},{1,0},{2,1},{3,2},{4,7},{5,4},{6,5},{7,6},{8,11},{9,8},{10,9... | collective-permute-start | bytes 786440 | tf_op jit(solution)/shard_map/ppermute | solution.py:328
  86.3 24.9 %all-to-all-start.2 = ((bf16[32,2,16,256]{3,2,1,0:T(8,128)(2,1)}), bf16[32,2,16,256]{3,2,1,0:T(8,128)(2,1)S(1)}, u32[]{:S(2)}, u32[]{:S(2)}) async-start(bf16[32,2,16,256]{3,2,1,0:T(8,128)(2,1)} %shard_map.161), calls=%async_computation.2 | async-start | bytes 1048576 | tf_op jit(solution)/shard_map/all_to_all | solution.py:302
  94.5 9.1 %collective-permute-start.7 = (bf16[256,512]{1,0:T(8,128)(2,1)S(1)}, bf16[256,512]{1,0:T(8,128)(2,1)S(1)}, u32[]{:S(2)}, u32[]{:S(2)}) collective-permute-start(bf16[256,512]{1,0:T(8,128)(2,1)S(1)} %get-tuple-element.48), channel_id=1, source_target_pairs={{0,2},{1,3},{2,0},{3,1},{4,6},{5,7},{6,4},{7,5},{8,10},{9,11},{10,... | collective-permute-start | bytes 786440 | tf_op jit(solution)/shard_map/ppermute | solution.py:328
  96.0 13.9 %collective-permute-start.8 = (bf16[256,512]{1,0:T(8,128)(2,1)S(1)}, bf16[256,512]{1,0:T(8,128)(2,1)S(1)}, u32[]{:S(2)}, u32[]{:S(2)}) collective-permute-start(bf16[256,512]{1,0:T(8,128)(2,1)S(1)} %get-tuple-element.49), channel_id=1, source_target_pairs={{0,1},{1,2},{2,3},{3,0},{4,5},{5,6},{6,7},{7,4},{8,9},{9,10},{10,1... | collective-permute-start | bytes 786440 | tf_op jit(solution)/shard_map/ppermute | solution.py:328
  96.0 13.9 %collective-permute-start.9 = (bf16[256,512]{1,0:T(8,128)(2,1)S(1)}, bf16[256,512]{1,0:T(8,128)(2,1)S(1)}, u32[]{:S(2)}, u32[]{:S(2)}) collective-permute-start(bf16[256,512]{1,0:T(8,128)(2,1)S(1)} %get-tuple-element.50), channel_id=1, source_target_pairs={{0,3},{1,0},{2,1},{3,2},{4,7},{5,4},{6,5},{7,6},{8,11},{9,8},{10,9... | collective-permute-start | bytes 786440 | tf_op jit(solution)/shard_map/ppermute | solution.py:328
  98.7 12.4 %copy-start = (bf16[256,512]{1,0:T(8,128)(2,1)S(1)}, bf16[256,512]{1,0:T(8,128)(2,1)}, u32[]{:S(2)}) copy-start(bf16[256,512]{1,0:T(8,128)(2,1)} %key_ref.1) | copy-start | bytes 786436
  98.7 12.4 %copy-start.1 = (bf16[256,512]{1,0:T(8,128)(2,1)S(1)}, bf16[256,512]{1,0:T(8,128)(2,1)}, u32[]{:S(2)}) copy-start(bf16[256,512]{1,0:T(8,128)(2,1)} %value_ref.1) | copy-start | bytes 786436
  100.0 10.3 %collective-permute-start.13 = (bf16[256,512]{1,0:T(8,128)(2,1)S(1)}, bf16[256,512]{1,0:T(8,128)(2,1)S(1)}, u32[]{:S(2)}, u32[]{:S(2)}) collective-permute-start(bf16[256,512]{1,0:T(8,128)(2,1)S(1)} %add_convert_fusion.1), channel_id=1, source_target_pairs={{0,4},{1,5},{2,6},{3,7},{4,0},{5,1},{6,2},{7,3},{8,12},{9,13},{10,... | collective-permute-start | bytes 786440 | tf_op jit(solution)/shard_map/ppermute | solution.py:328
